TPU v7x, 32 devices: a whole 2x2x4 slice. The times are simulated.
32 devices in a mesh: lat: 16 (over z, y, x), dp: 2 (over core).
Axes of the slice: x: 2, y: 2, z: 4, core: 2. Of those that a mesh axis runs over, the one named last changes fastest.
Arguments:
- state: float32 [2, 128, 256, 128], P('dp', 'lat'), may hold values from -6 to 6
- cotangent: float32 [2, 128, 256, 128], P('dp', 'lat'), may hold values from -0.18 to 0.18
- w_first: bfloat16 [128, 1024], replicated, may hold values from -0.5 to 0.5
- w_middle: bfloat16 [1024, 1024], replicated, may hold values from -0.1875 to 0.1875
- w_last: bfloat16 [1024, 128], replicated, may hold values from -0.1875 to 0.1875
Outputs:
- final_state: float32 [2, 128, 256, 128], P('dp', 'lat')
- grad_first: float32 [128, 1024], replicated
- grad_middle: float32 [1024, 1024], replicated
- grad_last: float32 [1024, 128], replicated
All inputs are finite; a program needn't handle non-finite values.
Results may differ from a plain program's by a relative error of at most 0.0048.
Values sent between devices are 32-bit elements; how exact they have to be, the bound alone decides.
A program may use at most 128 MiB of HBM per device.

v0:
```python
import functools
import math

import jax
import jax.numpy as jnp
import numpy as np
from jax import lax
from jax.experimental import pallas as pl
from jax.experimental.pallas import tpu as pltpu
from jax.sharding import PartitionSpec as P

MW = 64
STEPS = 2

high = lax.Precision.HIGH
tend_weight = 0.5


def grid_tables(lon_count, wave_count):
    lon_index = np.arange(lon_count)
    wave_index = np.arange(wave_count)
    angle = 2.0 * math.pi * (lon_index[:, None] * wave_index[None, :] % lon_count) / lon_count
    pair = np.stack([np.cos(angle), -np.sin(angle)], axis=2)
    factor = np.where(wave_index == 0, 1.0, 2.0)
    analysis = (pair / lon_count).reshape(lon_count, -1).astype(np.float32)
    synthesis = (pair * factor[None, :, None]).reshape(lon_count, -1).astype(np.float32)
    return analysis, synthesis


def legendre_tables(lat_count, wave_count):
    latitude = -0.5 * math.pi + (np.arange(lat_count) + 0.5) * math.pi / lat_count
    mu, cosine = np.sin(latitude), np.cos(latitude)
    quad_weight = cosine * math.pi / lat_count
    order = np.arange(wave_count, dtype=np.float64)
    steps = np.concatenate([[0.0], 0.5 * np.log((2 * order[1:] + 1) / (2 * order[1:]))])
    diagonal = np.exp(
        0.5 * math.log(0.5) + np.cumsum(steps)[:, None] + order[:, None] * np.log(cosine)[None, :]
    )
    rows = [diagonal]
    previous, current, ratio_prev = np.zeros_like(diagonal), diagonal, np.ones_like(order)
    for offset in range(1, wave_count):
        n = order + offset
        ratio = np.sqrt((4 * n * n - 1) / (n * n - order * order))
        following = ratio[:, None] * (mu[None, :] * current - previous / ratio_prev[:, None])
        previous, current, ratio_prev = current, following, ratio
        rows.append(following)
    table = np.stack(rows, axis=1)
    degree = order[:, None] + np.arange(wave_count)[None, :]
    kept = degree <= wave_count - 1
    damping = np.where(kept, 1.0 / (1.0 + degree * (degree + 1) / (wave_count * (wave_count - 1.0))), 0.0)
    table = np.where(kept[:, :, None], table, 0.0) * np.sqrt(damping)[:, :, None]
    return table.astype(np.float32), quad_weight.astype(np.float32)


def silu_pair(value):
    gate = 0.5 * jnp.tanh(0.5 * value) + 0.5
    hidden = value * gate
    return hidden, gate + hidden - hidden * gate


def forward_kernel(x_ref, w1_ref, w2_ref, w3_ref, moved_ref, h1_ref, s1_ref, h2_ref, s2_ref):
    field = x_ref[...]
    rows = field.astype(jnp.bfloat16)
    h1, s1 = silu_pair(jnp.dot(rows, w1_ref[...], preferred_element_type=jnp.float32))
    h1 = h1.astype(jnp.bfloat16)
    h1_ref[...] = h1
    s1_ref[...] = s1.astype(jnp.bfloat16)
    h2, s2 = silu_pair(jnp.dot(h1, w2_ref[...], preferred_element_type=jnp.float32))
    h2 = h2.astype(jnp.bfloat16)
    h2_ref[...] = h2
    s2_ref[...] = s2.astype(jnp.bfloat16)
    tend = jnp.dot(h2, w3_ref[...], preferred_element_type=jnp.float32)
    moved_ref[...] = field + tend_weight * tend


def forward_rows(x, w1, w2, w3):
    count, features = x.shape
    hidden = w1.shape[1]
    tile = math.gcd(count, 256)
    row = lambda width: pl.BlockSpec((tile, width), lambda i: (i, 0))
    whole = lambda w: pl.BlockSpec(w.shape, lambda i: (0, 0))
    wide = jax.ShapeDtypeStruct((count, hidden), jnp.bfloat16)
    return pl.pallas_call(
        forward_kernel,
        grid=(count // tile,),
        in_specs=[row(features), whole(w1), whole(w2), whole(w3)],
        out_specs=[row(features)] + [row(hidden)] * 4,
        out_shape=[jax.ShapeDtypeStruct(x.shape, jnp.float32)] + [wide] * 4,
        cost_estimate=pl.CostEstimate(
            flops=2 * count * (2 * features * hidden + hidden * hidden),
            bytes_accessed=count * hidden * 8, transcendentals=2 * count * hidden,
        ),
        compiler_params=pltpu.CompilerParams(dimension_semantics=("arbitrary",)),
    )(x, w1, w2, w3)


def mul_t(a, b):
    return lax.dot_general(a, b, (((1,), (1,)), ((), ())), preferred_element_type=jnp.float32)


def t_mul(a, b):
    return lax.dot_general(a, b, (((0,), (0,)), ((), ())), preferred_element_type=jnp.float32)


def backward_kernel(first_call, need_rows, *refs):
    p_ref, x_ref, h1_ref, s1_ref, h2_ref, s2_ref, w1_ref, w2_ref, w3_ref = refs[:9]
    refs = refs[9:]
    if not first_call:
        c1_ref, c2_ref, c3_ref = refs[:3]
        refs = refs[3:]
    g1_ref, g2_ref, g3_ref = refs[:3]

    @pl.when(pl.program_id(0) == 0)
    def _():
        if first_call:
            g1_ref[...] = jnp.zeros_like(g1_ref)
            g2_ref[...] = jnp.zeros_like(g2_ref)
            g3_ref[...] = jnp.zeros_like(g3_ref)
        else:
            g1_ref[...] = c1_ref[...]
            g2_ref[...] = c2_ref[...]
            g3_ref[...] = c3_ref[...]

    pulled = p_ref[...]
    gt = (tend_weight * pulled).astype(jnp.bfloat16)
    g3_ref[...] += t_mul(h2_ref[...], gt)
    ga2 = (mul_t(gt, w3_ref[...]) * s2_ref[...].astype(jnp.float32)).astype(jnp.bfloat16)
    g2_ref[...] += t_mul(h1_ref[...], ga2)
    ga1 = (mul_t(ga2, w2_ref[...]) * s1_ref[...].astype(jnp.float32)).astype(jnp.bfloat16)
    g1_ref[...] += t_mul(x_ref[...].astype(jnp.bfloat16), ga1)
    if need_rows:
        refs[3][...] = pulled + mul_t(ga1, w1_ref[...])


def backward_rows(pulled, x, saved, w1, w2, w3, carry, need_rows):
    count, features = x.shape
    hidden = w1.shape[1]
    tile = math.gcd(count, 512)
    row = lambda width: pl.BlockSpec((tile, width), lambda i: (i, 0))
    whole = lambda w: pl.BlockSpec(w.shape, lambda i: (0, 0))
    out_shape = [jax.ShapeDtypeStruct(w.shape, jnp.float32) for w in (w1, w2, w3)]
    out_specs = [whole(w) for w in (w1, w2, w3)]
    carried = [] if carry is None else list(carry)
    if need_rows:
        out_shape.append(jax.ShapeDtypeStruct(x.shape, jnp.float32))
        out_specs.append(row(features))
    return pl.pallas_call(
        functools.partial(backward_kernel, carry is None, need_rows),
        grid=(count // tile,),
        in_specs=[row(features)] * 2 + [row(hidden)] * 4
        + [whole(w) for w in (w1, w2, w3)] + [whole(c) for c in carried],
        out_specs=out_specs,
        out_shape=out_shape,
        cost_estimate=pl.CostEstimate(
            flops=4 * count * (2 * features * hidden + hidden * hidden),
            bytes_accessed=count * hidden * 8, transcendentals=0,
        ),
        compiler_params=pltpu.CompilerParams(dimension_semantics=("arbitrary",)),
    )(pulled, x, *saved, w1, w2, w3, *carried)


def body(state, cotangent, w1, w2, w3):
    sample, lat_rows, lon_count, features = state.shape
    bands = lax.axis_size("lat")
    lat_count = lat_rows * bands
    waves = MW // bands
    analysis, synthesis = grid_tables(lon_count, MW)
    table, quad = legendre_tables(lat_count, MW)
    mine = lax.dynamic_slice_in_dim(jnp.asarray(table), lax.axis_index("lat") * waves, waves, axis=0)
    base = jnp.einsum("mki,mkj->mij", mine, mine, precision=lax.Precision.HIGHEST)
    quad = jnp.asarray(quad)
    forward_op = base * quad[None, None, :]
    backward_op = base * quad[None, :, None]

    def spectral(parts):
        sent = []
        for field, first, _, _ in parts:
            wav = jnp.einsum("bjxf,xq->bqjf", field, first, precision=high)
            sent.append(wav.reshape(sample, bands, waves * 2, lat_rows, features))
        sent = jnp.concatenate(sent, axis=0).transpose(1, 0, 2, 3, 4)
        got = lax.all_to_all(sent, "lat", split_axis=0, concat_axis=0, tiled=True)
        got = got.reshape(bands, len(parts), sample, waves, 2, lat_rows, features)
        ops = jnp.stack([p[2] for p in parts]).reshape(len(parts), waves, bands, lat_rows, lat_count)
        got = got.transpose(1, 3, 0, 5, 2, 4, 6).reshape(len(parts), waves, lat_count, -1)
        ops = ops.reshape(len(parts), waves, lat_count, lat_count)
        back = jnp.einsum("smij,smjv->smiv", ops, got, precision=high)
        back = back.reshape(len(parts), waves, bands, lat_rows, sample, 2, features)
        back = back.transpose(2, 0, 4, 1, 5, 3, 6)
        back = lax.all_to_all(back, "lat", split_axis=0, concat_axis=0, tiled=True)
        out = []
        for index, (_, _, _, last) in enumerate(parts):
            piece = back[:, index].transpose(1, 0, 2, 3, 4, 5)
            piece = piece.reshape(sample, MW * 2, lat_rows, features)
            out.append(jnp.einsum("bqjf,xq->bjxf", piece, last, precision=high))
        return out

    flat = lambda field: field.reshape(sample * lat_rows * lon_count, features)
    x0 = flat(state)
    moved0, *saved0 = forward_rows(x0, w1, w2, w3)
    (pulled1,) = spectral([(cotangent, synthesis, backward_op, analysis)])
    (q1,) = spectral([(moved0.reshape(state.shape), analysis, forward_op, synthesis)])
    x1 = flat(q1)
    moved1, *saved1 = forward_rows(x1, w1, w2, w3)
    *totals, grad = backward_rows(flat(pulled1), x1, saved1, w1, w2, w3, None, True)
    (final,) = spectral([(moved1.reshape(state.shape), analysis, forward_op, synthesis)])
    (pulled0,) = spectral([(grad.reshape(state.shape), synthesis, backward_op, analysis)])
    totals = backward_rows(flat(pulled0), x0, saved0, w1, w2, w3, totals, False)
    totals = reduce_totals(totals)
    return (final, *totals)


def reduce_totals(totals):
    return lax.psum(tuple(totals), ("lat", "dp"))


def solution(mesh):
    field = P("dp", "lat", None, None)
    return jax.shard_map(
        body, mesh=mesh, in_specs=(field, field, P(), P(), P()),
        out_specs=(field, P(), P(), P()), check_vma=False,
    )
```

profile of v0, /device:TPU:1, one launch (start us, length us, event | category | flops | bytes accessed | tf_op | source)
XLA Modules:
  0.0 364.8 jit_solution(12545072260195943032)
XLA Ops:
  7.2 14.3 %shard_map.174 = (f32[2048,128]{1,0:T(8,128)}, bf16[2048,1024]{1,0:T(8,128)(2,1)}, bf16[2048,1024]{1,0:T(8,128)(2,1)}, bf16[2048,1024]{1,0:T(8,128)(2,1)}, bf16[2048,1024]{1,0:T(8,128)(2,1)}) custom-call(f32[2048,128]{1,0:T(8,128)} %bitcast.137, bf16[128,1024]{1,0:T(8,128)(2,1)} %refs_6_.3, bf16[1024,1024]{1,0:T(8,128)(2,1)} %refs_7_.3, ...), custom_call_target="tpu_custom_call" | custom-call | flops 5368709120 | bytes 16777216 | tf_op jit(solution)/shard_map/pallas_call | solution.py:83
  21.5 2.4 convolution_bitcast_fusion.8
  23.9 7.4 %all-to-all-start = ((f32[16,1,8,8,128]{4,2,3,1,0:T(8,128)}), f32[16,1,8,8,128]{4,2,3,1,0:T(8,128)S(1)}, u32[]{:S(2)}, u32[]{:S(2)}) async-start(f32[16,1,8,8,128]{4,2,3,1,0:T(8,128)} %convolution_bitcast_fusion.8), calls=%async_computation | async-start | bytes 1048576 | tf_op jit(solution)/shard_map/all_to_all | solution.py:181
  31.4 1.2 convolution_bitcast_fusion.4
  32.6 11.1 %all-to-all-done = f32[16,1,8,8,128]{4,2,3,1,0:T(8,128)S(1)} async-done(((f32[16,1,8,8,128]{4,2,3,1,0:T(8,128)}), f32[16,1,8,8,128]{4,2,3,1,0:T(8,128)S(1)}, u32[]{:S(2)}, u32[]{:S(2)}) %all-to-all-start) | async-done | bytes 524320 | tf_op jit(solution)/shard_map/all_to_all | solution.py:181
  43.7 6.0 %all-to-all-start.4 = ((f32[16,1,8,8,128]{4,2,3,1,0:T(8,128)}), f32[16,1,8,8,128]{4,2,3,1,0:T(8,128)S(1)}, u32[]{:S(2)}, u32[]{:S(2)}) async-start(f32[16,1,8,8,128]{4,2,3,1,0:T(8,128)} %convolution_bitcast_fusion.4), calls=%async_computation.4 | async-start | bytes 1048576 | tf_op jit(solution)/shard_map/all_to_all | solution.py:181
  49.7 1.6 fusion.17
  51.3 0.4 convolution_bitcast_fusion.7
  51.7 0.8 copy.68
  52.6 9.0 %all-to-all-done.4 = f32[16,1,8,8,128]{4,2,3,1,0:T(8,128)S(1)} async-done(((f32[16,1,8,8,128]{4,2,3,1,0:T(8,128)}), f32[16,1,8,8,128]{4,2,3,1,0:T(8,128)S(1)}, u32[]{:S(2)}, u32[]{:S(2)}) %all-to-all-start.4) | async-done | bytes 524320 | tf_op jit(solution)/shard_map/all_to_all | solution.py:181
  61.6 6.3 %all-to-all-start.1 = ((f32[16,1,1,4,2,8,128]{6,5,4,3,2,1,0:T(8,128)}), f32[16,1,1,4,2,8,128]{6,5,4,3,2,1,0:T(8,128)S(1)}, u32[]{:S(2)}, u32[]{:S(2)}) async-start(f32[16,1,1,4,2,8,128]{6,5,4,3,2,1,0:T(8,128)} %bitcast.119), calls=%async_computation.1 | async-start | bytes 1048576 | tf_op jit(solution)/shard_map/all_to_all | solution.py:189
  68.4 0.8 copy.66
  69.2 10.6 %all-to-all-done.1 = f32[16,1,1,4,2,8,128]{6,5,4,3,2,1,0:T(8,128)S(1)} async-done(((f32[16,1,1,4,2,8,128]{6,5,4,3,2,1,0:T(8,128)}), f32[16,1,1,4,2,8,128]{6,5,4,3,2,1,0:T(8,128)S(1)}, u32[]{:S(2)}, u32[]{:S(2)}) %all-to-all-start.1) | async-done | bytes 524320 | tf_op jit(solution)/shard_map/all_to_all | solution.py:189
  79.9 6.3 %all-to-all-start.5 = ((f32[16,1,1,4,2,8,128]{6,5,4,3,2,1,0:T(8,128)}), f32[16,1,1,4,2,8,128]{6,5,4,3,2,1,0:T(8,128)S(1)}, u32[]{:S(2)}, u32[]{:S(2)}) async-start(f32[16,1,1,4,2,8,128]{6,5,4,3,2,1,0:T(8,128)} %bitcast.117), calls=%async_computation.5 | async-start | bytes 1048576 | tf_op jit(solution)/shard_map/all_to_all | solution.py:189
  86.5 1.6 fusion.20
  88.1 14.3 %shard_map.175 = (f32[2048,128]{1,0:T(8,128)}, bf16[2048,1024]{1,0:T(8,128)(2,1)}, bf16[2048,1024]{1,0:T(8,128)(2,1)}, bf16[2048,1024]{1,0:T(8,128)(2,1)}, bf16[2048,1024]{1,0:T(8,128)(2,1)}) custom-call(f32[2048,128]{1,0:T(8,128)} %bitcast.131, bf16[128,1024]{1,0:T(8,128)(2,1)} %refs_6_.3, bf16[1024,1024]{1,0:T(8,128)(2,1)} %refs_7_.3, ...), custom_call_target="tpu_custom_call" | custom-call | flops 5368709120 | bytes 16777216 | tf_op jit(solution)/shard_map/pallas_call | solution.py:83
  102.6 1.5 fusion.21
  104.2 18.3 %shard_map.176 = (f32[128,1024]{1,0:T(8,128)}, f32[1024,1024]{1,0:T(8,128)}, f32[1024,128]{1,0:T(8,128)}, f32[2048,128]{1,0:T(8,128)}) custom-call(f32[2048,128]{1,0:T(8,128)} %bitcast.135, f32[2048,128]{1,0:T(8,128)} %bitcast.132, bf16[2048,1024]{1,0:T(8,128)(2,1)} %get-tuple-element.23.refs_2_, bf16[2048,1024]{1,0:T(8,128)(2,1)} %get-tuple-element.24.refs_3_, ...), custom_call_target="tpu_custom_call" | custom-call | flops 10737418240 | bytes 16777216 | tf_op jit(solution)/shard_map/pallas_call | solution.py:147
  122.5 1.6 convolution_bitcast_fusion.2
  124.1 17.2 %all_to_all.40 = f32[16,1,8,8,128]{4,2,3,1,0:T(8,128)S(1)} all-to-all(f32[16,1,8,8,128]{4,2,3,1,0:T(8,128)S(1)} %convolution_bitcast_fusion.2), channel_id=1, replica_groups=mesh['lat'=16,'dp'=2] {'lat'}, dimensions={0} | all-to-all | bytes 1048576 | tf_op jit(solution)/shard_map/all_to_all | solution.py:181
  141.9 17.4 %all_to_all.41 = f32[16,1,1,4,2,8,128]{6,5,4,3,2,1,0:T(8,128)S(1)} all-to-all(f32[16,1,1,4,2,8,128]{6,5,4,3,2,1,0:T(8,128)S(1)} %bitcast.128), channel_id=1, replica_groups=mesh['lat'=16,'dp'=2] {'lat'}, dimensions={0} | all-to-all | bytes 1048576 | tf_op jit(solution)/shard_map/all_to_all | solution.py:189
  159.6 1.5 fusion.22
  161.1 19.0 %shard_map.177 = (f32[128,1024]{1,0:T(8,128)}, f32[1024,1024]{1,0:T(8,128)}, f32[1024,128]{1,0:T(8,128)}) custom-call(f32[2048,128]{1,0:T(8,128)} %bitcast.133, f32[2048,128]{1,0:T(8,128)} %bitcast.138, bf16[2048,1024]{1,0:T(8,128)(2,1)} %get-tuple-element.28.refs_2_, bf16[2048,1024]{1,0:T(8,128)(2,1)} %get-tuple-element.29.refs_3_, ...), custom_call_target="tpu_custom_call" | custom-call | flops 10737418240 | bytes 16777216 | tf_op jit(solution)/shard_map/pallas_call | solution.py:147
  180.2 1.2 copy-done.2
  181.4 0.4 convolution_bitcast_fusion.6
  181.8 27.2 %all_to_all.42 = f32[16,1,8,8,128]{4,2,3,1,0:T(8,128)S(1)} all-to-all(f32[16,1,8,8,128]{4,2,3,1,0:T(8,128)S(1)} %convolution_bitcast_fusion.6), channel_id=1, replica_groups=mesh['lat'=16,'dp'=2] {'lat'}, dimensions={0} | all-to-all | bytes 1048576 | tf_op jit(solution)/shard_map/all_to_all | solution.py:181
  209.6 22.2 %all_to_all.43 = f32[16,1,1,4,2,8,128]{6,5,4,3,2,1,0:T(8,128)S(1)} all-to-all(f32[16,1,1,4,2,8,128]{6,5,4,3,2,1,0:T(8,128)S(1)} %bitcast.129), channel_id=1, replica_groups=mesh['lat'=16,'dp'=2] {'lat'}, dimensions={0} | all-to-all | bytes 1048576 | tf_op jit(solution)/shard_map/all_to_all | solution.py:189
  232.1 1.5 convolution_bitcast_fusion
  233.6 116.7 %all-reduce.3.cloned.1.call-done = (f32[128,1024]{1,0:T(8,128)}, f32[1024,1024]{1,0:T(8,128)}, f32[1024,128]{1,0:T(8,128)}) async-done(((f32[128,1024]{1,0:T(8,128)}, f32[1024,1024]{1,0:T(8,128)}, f32[1024,128]{1,0:T(8,128)}), (f32[128,1024]{1,0:T(8,128)}, f32[1024,1024]{1,0:T(8,128)}, f32[1024,128]{1,0:T(8,128)})) %all-reduce.3.cloned.1.call-update) | async-done | bytes 5242896 | tf_op jit(solution)/shard_map/psum | solution.py:213
  350.3 2.0 copy.72
  352.3 4.8 %copy.73 = f32[1024,1024]{1,0:T(8,128)} copy(f32[1024,1024]{1,0:T(8,128)} %get-tuple-element.43) | data formatting | bytes 8388608
  357.1 0.8 copy.74
  (29 shorter events, 2.6 us)
Async XLA Ops:
  7.2 24.2 %copy-start = (f32[1,8,256,128]{3,2,1,0:T(8,128)S(1)}, f32[1,8,256,128]{3,2,1,0:T(8,128)}, u32[]{:S(2)}) copy-start(f32[1,8,256,128]{3,2,1,0:T(8,128)} %param.16) | copy-start | bytes 3145732
  7.2 14.3 %copy-start.5 = (f32[16,8,256,1]{2,1,3,0:T(8,128)S(1)}, f32[16,8,256,1]{2,1,3,0:T(8,128)}, u32[]{:S(2)}) copy-start(f32[16,8,256,1]{2,1,3,0:T(8,128)} %constant.31) | copy-start | bytes 393220
  7.2 24.2 %copy-start.7 = (f32[16,8,256,1]{2,1,3,0:T(8,128)S(1)}, f32[16,8,256,1]{2,1,3,0:T(8,128)}, u32[]{:S(2)}) copy-start(f32[16,8,256,1]{2,1,3,0:T(8,128)} %constant.33) | copy-start | bytes 393220
  21.5 29.8 %copy-start.8 = (f32[128]{0:T(128)S(1)}, f32[128]{0:T(128)}, u32[]{:S(2)}) copy-start(f32[128]{0:T(128)} %constant.21.clone) | copy-start | bytes 1540
  23.9 19.7 %all-to-all-start = ((f32[16,1,8,8,128]{4,2,3,1,0:T(8,128)}), f32[16,1,8,8,128]{4,2,3,1,0:T(8,128)S(1)}, u32[]{:S(2)}, u32[]{:S(2)}) async-start(f32[16,1,8,8,128]{4,2,3,1,0:T(8,128)} %convolution_bitcast_fusion.8), calls=%async_computation | async-start | bytes 1048576 | tf_op jit(solution)/shard_map/all_to_all | solution.py:181
  43.7 17.9 %all-to-all-start.4 = ((f32[16,1,8,8,128]{4,2,3,1,0:T(8,128)}), f32[16,1,8,8,128]{4,2,3,1,0:T(8,128)S(1)}, u32[]{:S(2)}, u32[]{:S(2)}) async-start(f32[16,1,8,8,128]{4,2,3,1,0:T(8,128)} %convolution_bitcast_fusion.4), calls=%async_computation.4 | async-start | bytes 1048576 | tf_op jit(solution)/shard_map/all_to_all | solution.py:181
  49.7 36.8 %copy-start.4 = (f32[256,128,1]{1,0,2:T(8,128)S(1)}, f32[256,128,1]{1,0,2:T(8,128)}, u32[]{:S(2)}) copy-start(f32[256,128,1]{1,0,2:T(8,128)} %constant.30) | copy-start | bytes 393220
  61.6 18.2 %all-to-all-start.1 = ((f32[16,1,1,4,2,8,128]{6,5,4,3,2,1,0:T(8,128)}), f32[16,1,1,4,2,8,128]{6,5,4,3,2,1,0:T(8,128)S(1)}, u32[]{:S(2)}, u32[]{:S(2)}) async-start(f32[16,1,1,4,2,8,128]{6,5,4,3,2,1,0:T(8,128)} %bitcast.119), calls=%async_computation.1 | async-start | bytes 1048576 | tf_op jit(solution)/shard_map/all_to_all | solution.py:189
  79.9 22.5 %all-to-all-start.5 = ((f32[16,1,1,4,2,8,128]{6,5,4,3,2,1,0:T(8,128)}), f32[16,1,1,4,2,8,128]{6,5,4,3,2,1,0:T(8,128)S(1)}, u32[]{:S(2)}, u32[]{:S(2)}) async-start(f32[16,1,1,4,2,8,128]{6,5,4,3,2,1,0:T(8,128)} %bitcast.117), calls=%async_computation.5 | async-start | bytes 1048576 | tf_op jit(solution)/shard_map/all_to_all | solution.py:189
  86.2 264.1 %all-reduce.3.cloned.1.call-start = ((), (), s32[]{:S(2)}) async-start(), calls=%async_computation.8 | async-start | bytes 10485760 | tf_op jit(solution)/shard_map/psum | solution.py:213
  88.1 14.6 %copy-start.6 = (f32[256,128,1]{1,0,2:T(8,128)S(1)}, f32[256,128,1]{1,0,2:T(8,128)}, u32[]{:S(2)}) copy-start(f32[256,128,1]{1,0,2:T(8,128)} %constant.32) | copy-start | bytes 393220
  180.1 1.2 copy-start.2
  350.3 7.6 %copy-start.1 = (f32[1,8,256,128]{3,2,1,0:T(8,128)S(1)}, f32[1,8,256,128]{3,2,1,0:T(8,128)}, u32[]{:S(2)}) copy-start(f32[1,8,256,128]{3,2,1,0:T(8,128)} %param.16) | copy-start | bytes 3145732
  352.3 4.8 %copy-start.3 = (f32[1024,128]{1,0:T(8,128)S(1)}, f32[1024,128]{1,0:T(8,128)}, u32[]{:S(2)}) copy-start(f32[1024,128]{1,0:T(8,128)} %get-tuple-element.44) | copy-start | bytes 1572868
Sparse Core Ops, SparseCore 0:
  180.3 169.9 all-reduce.2
where the time goes:
time: 368 us; the launch traced here: 365 us
  waiting for transfers between devices  147 us (40%)
  blocking collectives  84.1 us (23%)
  Pallas kernels  65.8 us (18%)
  starting transfers between devices  26 us (7%)
  matrix products  15.3 us (4%)
  between operations  14.3 us (4%)
  local copies, waits for them, and re-layouts  11.7 us (3%)
    psum x1, waiting for transfers between devices, reduce_totals(): return lax.psum(tuple(totals), ('lat', 'dp'))  117 us
    all_to_all x2, blocking collectives, spectral(): got = lax.all_to_all(sent, 'lat', split_axis=0, concat_axis=0, tiled=True)  44.5 us
    all_to_all x2, blocking collectives, spectral(): back = lax.all_to_all(back, 'lat', split_axis=0, concat_axis=0, tiled=True)  39.7 us
    pallas_call x2, Pallas kernels, backward_rows(): pl.pallas_call(functools.partial(backward_kernel, carry is None, need_row...  37.3 us
    pallas_call x2, Pallas kernels, forward_rows(): pl.pallas_call(forward_kernel, grid=(count // tile,), in_specs=[row(featu...  28.5 us
    all_to_all x2, waiting for transfers between devices, spectral(): got = lax.all_to_all(sent, 'lat', split_axis=0, concat_axis=0, tiled=True)  20.1 us
    all_to_all x2, starting transfers between devices, spectral(): got = lax.all_to_all(sent, 'lat', split_axis=0, concat_axis=0, tiled=True)  13.4 us
    all_to_all x2, starting transfers between devices, spectral(): back = lax.all_to_all(back, 'lat', split_axis=0, concat_axis=0, tiled=True)  12.6 us
  transfers between devices with their start and end apart: 5, of which 4 were waited for; matrix products, arithmetic and copies ran while one was open for 3% of the time, Pallas kernels for 4%

commit v1 on v0

--- a/solution.py
+++ b/solution.py
@@ -159,6 +159,222 @@
     )(pulled, x, *saved, w1, w2, w3, *carried)
 
 
+MESH_ID = pl.DeviceIdType.MESH
+LANES = 128
+CHUNK = 1024
+
+
+class Place:
+    def __init__(self, bands):
+        self.me = lax.axis_index("lat")
+        self.core = lax.axis_index("dp")
+        self.depth = bands // 4
+        self.x = lax.rem(self.me, 2)
+        self.y = lax.rem(self.me // 2, 2)
+        self.z = self.me // 4
+        self.across_core = {"dp": 1 - self.core}
+        self.across_x = {"lat": self.me + 1 - 2 * self.x}
+        self.across_y = {"lat": self.me + 2 - 4 * self.y}
+
+    def along_z(self, step):
+        layer = lax.rem(self.z + step, self.depth)
+        return layer, {"lat": layer * 4 + lax.rem(self.me, 4)}
+
+
+def signal_to(device):
+    pl.semaphore_signal(pltpu.get_barrier_semaphore(), inc=1, device_id=device, device_id_type=MESH_ID)
+
+
+def greet_reduce(place):
+    signal_to(place.across_core)
+    signal_to(place.across_x)
+    signal_to(place.across_y)
+    for step in range(1, place.depth):
+        signal_to(place.along_z(step)[1])
+    pl.semaphore_wait(pltpu.get_barrier_semaphore(), place.depth + 2)
+
+
+def send(src, dst, ssem, rsem, device):
+    pltpu.make_async_remote_copy(
+        src_ref=src, dst_ref=dst, send_sem=ssem, recv_sem=rsem, device_id=device, device_id_type=MESH_ID
+    ).start()
+
+
+def wait_bytes(ref, sem):
+    pltpu.make_async_copy(ref, ref, sem).wait()
+
+
+class Reduce:
+    SENDS = 8
+
+    @staticmethod
+    def scratch(chunks, depth):
+        rows = lambda count: pltpu.VMEM((chunks * count, LANES), jnp.float32)
+        sems = lambda *dims: pltpu.SemaphoreType.DMA((chunks,) + dims)
+        return [
+            rows(CHUNK), rows(CHUNK), rows(512), rows(256), rows(128),
+            pltpu.VMEM((chunks, depth - 1, 256 // depth // 2, LANES), jnp.float32),
+            sems(), sems(2), sems(2), sems(depth - 1), sems(depth - 1), sems(2), sems(2), sems(),
+            pltpu.SemaphoreType.DMA((Reduce.SENDS,)),
+        ]
+
+    def __init__(self, place, chunks, refs):
+        (self.g, self.o, self.r0, self.r1, self.r2, self.r3,
+         self.d0, self.m1, self.m2, self.z3, self.z4, self.m5, self.m6, self.d7, self.sent) = refs
+        self.place, self.chunks = place, chunks
+        self.piece = 64 // place.depth
+        p = place
+        half = p.core * 512
+        self.first = ((p.across_x, p.x), (p.across_y, p.y))
+        self.second = (self.first[1], self.first[0])
+        self.quarter = (half, half + 256)
+        self.eighth = tuple(self.quarter[i] + self.first[i][1] * 128 for i in (0, 1))
+        self.sixteenth = tuple(self.eighth[i] + self.second[i][1] * 64 for i in (0, 1))
+        self.own = tuple(self.sixteenth[i] + p.z * self.piece for i in (0, 1))
+
+    def rows(self, ref, k, offset, count, span=CHUNK):
+        return ref.at[pl.ds(pl.multiple_of(k * span + offset, 8), count), :]
+
+    def stage0(self, k):
+        other = (1 - self.place.core) * 512
+        send(self.rows(self.g, k, other, 512), self.rows(self.r0, k, 0, 512, 512),
+             self.sent.at[0], self.d0.at[k], self.place.across_core)
+
+    def stage1(self, k):
+        wait_bytes(self.rows(self.r0, k, 0, 512, 512), self.d0.at[k])
+        mine = self.rows(self.g, k, self.place.core * 512, 512)
+        mine[...] += self.rows(self.r0, k, 0, 512, 512)[...]
+        for i in (0, 1):
+            device, bit = self.first[i]
+            send(self.rows(self.g, k, self.quarter[i] + (1 - bit) * 128, 128),
+                 self.rows(self.r1, k, i * 128, 128, 256), self.sent.at[1], self.m1.at[k, i], device)
+
+    def stage2(self, k):
+        for i in (0, 1):
+            got = self.rows(self.r1, k, i * 128, 128, 256)
+            wait_bytes(got, self.m1.at[k, i])
+            self.rows(self.g, k, self.eighth[i], 128)[...] += got[...]
+        for i in (0, 1):
+            device, bit = self.second[i]
+            send(self.rows(self.g, k, self.eighth[i] + (1 - bit) * 64, 64),
+                 self.rows(self.r2, k, i * 64, 64, 128), self.sent.at[2], self.m2.at[k, i], device)
+
+    def stage3(self, k):
+        for i in (0, 1):
+            got = self.rows(self.r2, k, i * 64, 64, 128)
+            wait_bytes(got, self.m2.at[k, i])
+            self.rows(self.g, k, self.sixteenth[i], 64)[...] += got[...]
+        for step in range(1, self.place.depth):
+            layer, device = self.place.along_z(step)
+            for i in (0, 1):
+                send(self.rows(self.g, k, self.sixteenth[i] + layer * self.piece, self.piece),
+                     self.r3.at[k, step - 1, pl.ds(i * self.piece, self.piece), :],
+                     self.sent.at[3], self.z3.at[k, step - 1], device)
+
+    def stage4(self, k):
+        total = [self.rows(self.g, k, self.own[i], self.piece)[...] for i in (0, 1)]
+        for step in range(1, self.place.depth):
+            wait_bytes(self.r3.at[k, step - 1], self.z3.at[k, step - 1])
+            for i in (0, 1):
+                total[i] += self.r3[k, step - 1, pl.ds(i * self.piece, self.piece), :]
+        for i in (0, 1):
+            self.rows(self.o, k, self.own[i], self.piece)[...] = total[i]
+        for step in range(1, self.place.depth):
+            _, device = self.place.along_z(step)
+            for i in (0, 1):
+                mine = self.rows(self.o, k, self.own[i], self.piece)
+                send(mine, mine, self.sent.at[4], self.z4.at[k, step - 1], device)
+
+    def stage5(self, k):
+        for step in range(1, self.place.depth):
+            wait_bytes(self.r3.at[k, step - 1], self.z4.at[k, step - 1])
+        for i in (0, 1):
+            mine = self.rows(self.o, k, self.sixteenth[i], 64)
+            send(mine, mine, self.sent.at[5], self.m5.at[k, i], self.second[i][0])
+
+    def stage6(self, k):
+        for i in (0, 1):
+            wait_bytes(self.rows(self.r2, k, 0, 64, 128), self.m5.at[k, i])
+        for i in (0, 1):
+            mine = self.rows(self.o, k, self.eighth[i], 128)
+            send(mine, mine, self.sent.at[6], self.m6.at[k, i], self.first[i][0])
+
+    def stage7(self, k):
+        for i in (0, 1):
+            wait_bytes(self.rows(self.r1, k, 0, 128, 256), self.m6.at[k, i])
+        mine = self.rows(self.o, k, self.place.core * 512, 512)
+        send(mine, mine, self.sent.at[7], self.d7.at[k], self.place.across_core)
+
+    def stage8(self, k):
+        wait_bytes(self.rows(self.r0, k, 0, 512, 512), self.d7.at[k])
+
+    def step(self, t):
+        stages = [self.stage0, self.stage1, self.stage2, self.stage3, self.stage4,
+                  self.stage5, self.stage6, self.stage7, self.stage8]
+        for lag in range(8, -1, -1):
+            k = t - lag
+
+            @pl.when(jnp.logical_and(k >= 0, k < self.chunks))
+            def _(k=k, lag=lag):
+                stages[lag](k)
+
+    @property
+    def steps(self):
+        return self.chunks + 8
+
+    def drain(self):
+        counts = [512, 256, 128, 2 * self.piece * (self.place.depth - 1)]
+        counts = counts + counts[::-1]
+        for i, count in enumerate(counts):
+            wait_bytes(self.g.at[pl.ds(0, count * self.chunks), :], self.sent.at[i])
+
+
+def reduce_kernel(bands, g1_ref, g2_ref, g3_ref, o1_ref, o2_ref, o3_ref, *scratch):
+    place = Place(bands)
+    hidden = g2_ref.shape[1]
+    blocks = hidden // LANES
+    chunks = blocks + 2
+    red = Reduce(place, chunks, scratch)
+    greet_reduce(place)
+
+    for b in range(blocks):
+        red.g[pl.ds(b * CHUNK, CHUNK), :] = g2_ref[:, pl.ds(b * LANES, LANES)]
+        red.g[pl.ds((blocks + 1) * CHUNK + b * LANES, LANES), :] = g1_ref[:, pl.ds(b * LANES, LANES)]
+    red.g[pl.ds(blocks * CHUNK, CHUNK), :] = g3_ref[...]
+
+    @pl.loop(0, red.steps)
+    def _(t):
+        red.step(t)
+
+    for b in range(blocks):
+        o2_ref[:, pl.ds(b * LANES, LANES)] = red.o[pl.ds(b * CHUNK, CHUNK), :]
+        o1_ref[:, pl.ds(b * LANES, LANES)] = red.o[pl.ds((blocks + 1) * CHUNK + b * LANES, LANES), :]
+    o3_ref[...] = red.o[pl.ds(blocks * CHUNK, CHUNK), :]
+    red.drain()
+
+
+def fits_reduce(bands, pairs, features, hidden):
+    return pairs == 2 and bands % 8 == 0 and bands <= 32 and features == LANES and hidden == CHUNK
+
+
+def reduce_totals(totals):
+    bands, pairs = lax.axis_size("lat"), lax.axis_size("dp")
+    features, hidden = totals[0].shape
+    if not fits_reduce(bands, pairs, features, hidden):
+        return lax.psum(tuple(totals), ("lat", "dp"))
+    vmem = pl.BlockSpec(memory_space=pltpu.VMEM)
+    return pl.pallas_call(
+        functools.partial(reduce_kernel, bands),
+        in_specs=[vmem] * 3,
+        out_specs=[vmem] * 3,
+        out_shape=[jax.ShapeDtypeStruct(t.shape, t.dtype) for t in totals],
+        scratch_shapes=Reduce.scratch(hidden // LANES + 2, bands // 4),
+        compiler_params=pltpu.CompilerParams(
+            collective_id=3, has_side_effects=True, vmem_limit_bytes=56 * 2**20
+        ),
+    )(*totals)
+
+
 def body(state, cotangent, w1, w2, w3):
     sample, lat_rows, lon_count, features = state.shape
     bands = lax.axis_size("lat")
@@ -209,10 +425,6 @@
     return (final, *totals)
 
 
-def reduce_totals(totals):
-    return lax.psum(tuple(totals), ("lat", "dp"))
-
-
 def solution(mesh):
     field = P("dp", "lat", None, None)
     return jax.shard_map(

time: 368 us -> 287 us (0.78)
  waiting for transfers between devices: 147 us -> 58.8 us
  blocking collectives: 84.1 us -> 0 us
  Pallas kernels: 65.8 us -> 144 us
  starting transfers between devices: 26 us -> 52.3 us
  between operations: 14.3 us -> 0.89 us
    psum x1 -> x0, waiting for transfers between devices: 117 us -> none  [reduce_totals(): return lax.psum(tuple(totals), ('lat', 'dp'))]
    all_to_all x4 -> x0, blocking collectives: 84.1 us -> none  [the longest x2 44.5 us: spectral(): got = lax.all_to_all(sent, 'lat', split_axis=0, concat_axis=0, tiled=True)]
    pallas_call x0 -> x1, Pallas kernels: none -> 77.8 us  [reduce_totals(): pl.pallas_call(functools.partial(reduce_kernel, bands), in_specs=[vmem] *...]
    all_to_all x2 -> x4, waiting for transfers between devices: 10.6 us -> 29.5 us  [spectral(): back = lax.all_to_all(back, 'lat', split_axis=0, concat_axis=0, tiled=True)]
    all_to_all x2 -> x4, starting transfers between devices: 12.6 us -> 26.3 us  [spectral(): back = lax.all_to_all(back, 'lat', split_axis=0, concat_axis=0, tiled=True)]
    all_to_all x2 -> x4, starting transfers between devices: 13.4 us -> 26.1 us  [spectral(): got = lax.all_to_all(sent, 'lat', split_axis=0, concat_axis=0, tiled=True)]
    all_to_all x2 -> x4, waiting for transfers between devices: 20.1 us -> 29.3 us  [spectral(): got = lax.all_to_all(sent, 'lat', split_axis=0, concat_axis=0, tiled=True)]
    unnamed x21 -> x19, local copies, waits for them, and re-layouts: 8.85 us -> 7.66 us
  transfers between devices with their start and end apart: 5 -> 8, of which waited for: 4 -> 6; matrix products, arithmetic and copies ran while one was open for 3% -> 6% of each run, Pallas kernels for 4% -> 11%
where the time goes in v1:
time: 287 us; the launch traced here: 286 us
  Pallas kernels  144 us (50%)
  waiting for transfers between devices  58.8 us (20%)
  starting transfers between devices  52.3 us (18%)
  matrix products  18.2 us (6%)
  local copies, waits for them, and re-layouts  12.1 us (4%)
    pallas_call x1, Pallas kernels, reduce_totals(): pl.pallas_call(functools.partial(reduce_kernel, bands), in_specs=[vmem] *...  77.8 us
    pallas_call x2, Pallas kernels, backward_rows(): pl.pallas_call(functools.partial(backward_kernel, carry is None, need_row...  37.3 us
    all_to_all x4, waiting for transfers between devices, spectral(): back = lax.all_to_all(back, 'lat', split_axis=0, concat_axis=0, tiled=True)  29.5 us
    all_to_all x4, waiting for transfers between devices, spectral(): got = lax.all_to_all(sent, 'lat', split_axis=0, concat_axis=0, tiled=True)  29.3 us
    pallas_call x2, Pallas kernels, forward_rows(): pl.pallas_call(forward_kernel, grid=(count // tile,), in_specs=[row(featu...  28.5 us
    all_to_all x4, starting transfers between devices, spectral(): back = lax.all_to_all(back, 'lat', split_axis=0, concat_axis=0, tiled=True)  26.3 us
    all_to_all x4, starting transfers between devices, spectral(): got = lax.all_to_all(sent, 'lat', split_axis=0, concat_axis=0, tiled=True)  26.1 us
    dot_general x4, matrix products, spectral(): wav = jnp.einsum('bjxf,xq->bqjf', field, first, precision=high)  8.53 us
  transfers between devices with their start and end apart: 8, of which 6 were waited for; matrix products, arithmetic and copies ran while one was open for 6% of the time, Pallas kernels for 11%

profile of v1, /device:TPU:1, one launch (start us, length us, event | category | flops | bytes accessed | tf_op | source)
XLA Modules:
  0.0 286.0 jit_solution(18266248337972409801)
XLA Ops:
  0.7 14.3 %shard_map.174 = (f32[2048,128]{1,0:T(8,128)}, bf16[2048,1024]{1,0:T(8,128)(2,1)}, bf16[2048,1024]{1,0:T(8,128)(2,1)}, bf16[2048,1024]{1,0:T(8,128)(2,1)}, bf16[2048,1024]{1,0:T(8,128)(2,1)}) custom-call(f32[2048,128]{1,0:T(8,128)} %bitcast.135, bf16[128,1024]{1,0:T(8,128)(2,1)} %refs_6_.3, bf16[1024,1024]{1,0:T(8,128)(2,1)} %refs_7_.3, ...), custom_call_target="tpu_custom_call" | custom-call | flops 5368709120 | bytes 16777216 | tf_op jit(solution)/shard_map/pallas_call | solution.py:83
  15.0 2.4 convolution_bitcast_fusion.8
  17.4 7.4 %all-to-all-start = ((f32[16,1,8,8,128]{4,2,3,1,0:T(8,128)}), f32[16,1,8,8,128]{4,2,3,1,0:T(8,128)S(1)}, u32[]{:S(2)}, u32[]{:S(2)}) async-start(f32[16,1,8,8,128]{4,2,3,1,0:T(8,128)} %convolution_bitcast_fusion.8), calls=%async_computation | async-start | bytes 1048576 | tf_op jit(solution)/shard_map/all_to_all | solution.py:397
  24.8 1.2 convolution_bitcast_fusion.4
  26.0 11.1 %all-to-all-done = f32[16,1,8,8,128]{4,2,3,1,0:T(8,128)S(1)} async-done(((f32[16,1,8,8,128]{4,2,3,1,0:T(8,128)}), f32[16,1,8,8,128]{4,2,3,1,0:T(8,128)S(1)}, u32[]{:S(2)}, u32[]{:S(2)}) %all-to-all-start) | async-done | bytes 524320 | tf_op jit(solution)/shard_map/all_to_all | solution.py:397
  37.1 6.0 %all-to-all-start.4 = ((f32[16,1,8,8,128]{4,2,3,1,0:T(8,128)}), f32[16,1,8,8,128]{4,2,3,1,0:T(8,128)S(1)}, u32[]{:S(2)}, u32[]{:S(2)}) async-start(f32[16,1,8,8,128]{4,2,3,1,0:T(8,128)} %convolution_bitcast_fusion.4), calls=%async_computation.4 | async-start | bytes 1048576 | tf_op jit(solution)/shard_map/all_to_all | solution.py:397
  43.1 1.6 fusion.17
  46.1 9.0 %all-to-all-done.4 = f32[16,1,8,8,128]{4,2,3,1,0:T(8,128)S(1)} async-done(((f32[16,1,8,8,128]{4,2,3,1,0:T(8,128)}), f32[16,1,8,8,128]{4,2,3,1,0:T(8,128)S(1)}, u32[]{:S(2)}, u32[]{:S(2)}) %all-to-all-start.4) | async-done | bytes 524320 | tf_op jit(solution)/shard_map/all_to_all | solution.py:397
  55.1 6.3 %all-to-all-start.1 = ((f32[16,1,1,4,2,8,128]{6,5,4,3,2,1,0:T(8,128)}), f32[16,1,1,4,2,8,128]{6,5,4,3,2,1,0:T(8,128)S(1)}, u32[]{:S(2)}, u32[]{:S(2)}) async-start(f32[16,1,1,4,2,8,128]{6,5,4,3,2,1,0:T(8,128)} %bitcast.119), calls=%async_computation.1 | async-start | bytes 1048576 | tf_op jit(solution)/shard_map/all_to_all | solution.py:405
  61.8 0.9 copy.66
  62.7 10.6 %all-to-all-done.1 = f32[16,1,1,4,2,8,128]{6,5,4,3,2,1,0:T(8,128)S(1)} async-done(((f32[16,1,1,4,2,8,128]{6,5,4,3,2,1,0:T(8,128)}), f32[16,1,1,4,2,8,128]{6,5,4,3,2,1,0:T(8,128)S(1)}, u32[]{:S(2)}, u32[]{:S(2)}) %all-to-all-start.1) | async-done | bytes 524320 | tf_op jit(solution)/shard_map/all_to_all | solution.py:405
  73.3 6.3 %all-to-all-start.5 = ((f32[16,1,1,4,2,8,128]{6,5,4,3,2,1,0:T(8,128)}), f32[16,1,1,4,2,8,128]{6,5,4,3,2,1,0:T(8,128)S(1)}, u32[]{:S(2)}, u32[]{:S(2)}) async-start(f32[16,1,1,4,2,8,128]{6,5,4,3,2,1,0:T(8,128)} %bitcast.117), calls=%async_computation.5 | async-start | bytes 1048576 | tf_op jit(solution)/shard_map/all_to_all | solution.py:405
  79.9 1.5 fusion.20
  81.5 14.3 %shard_map.175 = (f32[2048,128]{1,0:T(8,128)}, bf16[2048,1024]{1,0:T(8,128)(2,1)}, bf16[2048,1024]{1,0:T(8,128)(2,1)}, bf16[2048,1024]{1,0:T(8,128)(2,1)}, bf16[2048,1024]{1,0:T(8,128)(2,1)}) custom-call(f32[2048,128]{1,0:T(8,128)} %bitcast.128, bf16[128,1024]{1,0:T(8,128)(2,1)} %refs_6_.3, bf16[1024,1024]{1,0:T(8,128)(2,1)} %refs_7_.3, ...), custom_call_target="tpu_custom_call" | custom-call | flops 5368709120 | bytes 16777216 | tf_op jit(solution)/shard_map/pallas_call | solution.py:83
  95.7 2.4 convolution_bitcast_fusion.6
  98.2 6.4 %all-to-all-start.2 = ((f32[16,1,8,8,128]{4,2,3,1,0:T(8,128)}), f32[16,1,8,8,128]{4,2,3,1,0:T(8,128)S(1)}, u32[]{:S(2)}, u32[]{:S(2)}) async-start(f32[16,1,8,8,128]{4,2,3,1,0:T(8,128)} %convolution_bitcast_fusion.6), calls=%async_computation.2 | async-start | bytes 1048576 | tf_op jit(solution)/shard_map/all_to_all | solution.py:397
  104.8 1.6 fusion.21
  106.4 18.3 %shard_map.176 = (f32[128,1024]{1,0:T(8,128)}, f32[1024,1024]{1,0:T(8,128)}, f32[1024,128]{1,0:T(8,128)}, f32[2048,128]{1,0:T(8,128)}) custom-call(f32[2048,128]{1,0:T(8,128)} %bitcast.131, f32[2048,128]{1,0:T(8,128)} %bitcast.129, bf16[2048,1024]{1,0:T(8,128)(2,1)} %get-tuple-element.26.refs_2_, bf16[2048,1024]{1,0:T(8,128)(2,1)} %get-tuple-element.27.refs_3_, ...), custom_call_target="tpu_custom_call" | custom-call | flops 10737418240 | bytes 16777216 | tf_op jit(solution)/shard_map/pallas_call | solution.py:147
  124.7 2.4 convolution_bitcast_fusion.2
  127.1 6.3 %all-to-all-start.6 = ((f32[16,1,8,8,128]{4,2,3,1,0:T(8,128)}), f32[16,1,8,8,128]{4,2,3,1,0:T(8,128)S(1)}, u32[]{:S(2)}, u32[]{:S(2)}) async-start(f32[16,1,8,8,128]{4,2,3,1,0:T(8,128)} %convolution_bitcast_fusion.2), calls=%async_computation.6 | async-start | bytes 1048576 | tf_op jit(solution)/shard_map/all_to_all | solution.py:397
  134.8 9.2 %all-to-all-done.6 = f32[16,1,8,8,128]{4,2,3,1,0:T(8,128)S(1)} async-done(((f32[16,1,8,8,128]{4,2,3,1,0:T(8,128)}), f32[16,1,8,8,128]{4,2,3,1,0:T(8,128)S(1)}, u32[]{:S(2)}, u32[]{:S(2)}) %all-to-all-start.6) | async-done | bytes 524320 | tf_op jit(solution)/shard_map/all_to_all | solution.py:397
  144.0 7.1 %all-to-all-start.3 = ((f32[16,1,1,4,2,8,128]{6,5,4,3,2,1,0:T(8,128)}), f32[16,1,1,4,2,8,128]{6,5,4,3,2,1,0:T(8,128)S(1)}, u32[]{:S(2)}, u32[]{:S(2)}) async-start(f32[16,1,1,4,2,8,128]{6,5,4,3,2,1,0:T(8,128)} %bitcast.118), calls=%async_computation.3 | async-start | bytes 1048576 | tf_op jit(solution)/shard_map/all_to_all | solution.py:405
  151.6 0.9 copy.65
  152.4 9.7 %all-to-all-done.3 = f32[16,1,1,4,2,8,128]{6,5,4,3,2,1,0:T(8,128)S(1)} async-done(((f32[16,1,1,4,2,8,128]{6,5,4,3,2,1,0:T(8,128)}), f32[16,1,1,4,2,8,128]{6,5,4,3,2,1,0:T(8,128)S(1)}, u32[]{:S(2)}, u32[]{:S(2)}) %all-to-all-start.3) | async-done | bytes 524320 | tf_op jit(solution)/shard_map/all_to_all | solution.py:405
  162.1 6.5 %all-to-all-start.7 = ((f32[16,1,1,4,2,8,128]{6,5,4,3,2,1,0:T(8,128)}), f32[16,1,1,4,2,8,128]{6,5,4,3,2,1,0:T(8,128)S(1)}, u32[]{:S(2)}, u32[]{:S(2)}) async-start(f32[16,1,1,4,2,8,128]{6,5,4,3,2,1,0:T(8,128)} %bitcast.116), calls=%async_computation.7 | async-start | bytes 1048576 | tf_op jit(solution)/shard_map/all_to_all | solution.py:405
  169.0 1.6 convolution_bitcast_fusion
  170.5 9.2 %all-to-all-done.7 = f32[16,1,1,4,2,8,128]{6,5,4,3,2,1,0:T(8,128)S(1)} async-done(((f32[16,1,1,4,2,8,128]{6,5,4,3,2,1,0:T(8,128)}), f32[16,1,1,4,2,8,128]{6,5,4,3,2,1,0:T(8,128)S(1)}, u32[]{:S(2)}, u32[]{:S(2)}) %all-to-all-start.7) | async-done | bytes 524320 | tf_op jit(solution)/shard_map/all_to_all | solution.py:405
  180.0 1.6 fusion.22
  181.6 19.0 %shard_map.177 = (f32[128,1024]{1,0:T(8,128)}, f32[1024,1024]{1,0:T(8,128)}, f32[1024,128]{1,0:T(8,128)}) custom-call(f32[2048,128]{1,0:T(8,128)} %bitcast.130, f32[2048,128]{1,0:T(8,128)} %bitcast.136, bf16[2048,1024]{1,0:T(8,128)(2,1)} %get-tuple-element.31.refs_2_, bf16[2048,1024]{1,0:T(8,128)(2,1)} %get-tuple-element.32.refs_3_, ...), custom_call_target="tpu_custom_call" | custom-call | flops 10737418240 | bytes 16777216 | tf_op jit(solution)/shard_map/pallas_call | solution.py:147
  200.6 77.8 %shard_map.178 = (f32[128,1024]{1,0:T(8,128)}, f32[1024,1024]{1,0:T(8,128)}, f32[1024,128]{1,0:T(8,128)}) custom-call(f32[128,1024]{1,0:T(8,128)} %get-tuple-element.38.g1_ref, f32[1024,1024]{1,0:T(8,128)} %get-tuple-element.39.g2_ref, f32[1024,128]{1,0:T(8,128)} %get-tuple-element.40.g3_ref), custom_call_target="tpu_custom_call" | custom-call | tf_op jit(solution)/shard_map/pallas_call | solution.py:366
  278.4 2.0 copy.72
  280.4 4.8 %copy.73 = f32[1024,1024]{1,0:T(8,128)} copy(f32[1024,1024]{1,0:T(8,128)} %get-tuple-element.50) | data formatting | bytes 8388608
  (29 shorter events, 5.4 us)
Async XLA Ops:
  0.6 24.2 %copy-start = (f32[1,8,256,128]{3,2,1,0:T(8,128)S(1)}, f32[1,8,256,128]{3,2,1,0:T(8,128)}, u32[]{:S(2)}) copy-start(f32[1,8,256,128]{3,2,1,0:T(8,128)} %param.16) | copy-start | bytes 3145732
  0.6 14.3 %copy-start.6 = (f32[16,8,256,1]{2,1,3,0:T(8,128)S(1)}, f32[16,8,256,1]{2,1,3,0:T(8,128)}, u32[]{:S(2)}) copy-start(f32[16,8,256,1]{2,1,3,0:T(8,128)} %constant.31) | copy-start | bytes 393220
  0.7 24.2 %copy-start.5 = (f32[16,8,256,1]{2,1,3,0:T(8,128)S(1)}, f32[16,8,256,1]{2,1,3,0:T(8,128)}, u32[]{:S(2)}) copy-start(f32[16,8,256,1]{2,1,3,0:T(8,128)} %constant.33) | copy-start | bytes 393220
  14.9 29.8 %copy-start.7 = (f32[128]{0:T(128)S(1)}, f32[128]{0:T(128)}, u32[]{:S(2)}) copy-start(f32[128]{0:T(128)} %constant.21.clone) | copy-start | bytes 1540
  17.4 19.7 %all-to-all-start = ((f32[16,1,8,8,128]{4,2,3,1,0:T(8,128)}), f32[16,1,8,8,128]{4,2,3,1,0:T(8,128)S(1)}, u32[]{:S(2)}, u32[]{:S(2)}) async-start(f32[16,1,8,8,128]{4,2,3,1,0:T(8,128)} %convolution_bitcast_fusion.8), calls=%async_computation | async-start | bytes 1048576 | tf_op jit(solution)/shard_map/all_to_all | solution.py:397
  37.1 17.9 %all-to-all-start.4 = ((f32[16,1,8,8,128]{4,2,3,1,0:T(8,128)}), f32[16,1,8,8,128]{4,2,3,1,0:T(8,128)S(1)}, u32[]{:S(2)}, u32[]{:S(2)}) async-start(f32[16,1,8,8,128]{4,2,3,1,0:T(8,128)} %convolution_bitcast_fusion.4), calls=%async_computation.4 | async-start | bytes 1048576 | tf_op jit(solution)/shard_map/all_to_all | solution.py:397
  43.1 36.8 %copy-start.4 = (f32[256,128,1]{1,0,2:T(8,128)S(1)}, f32[256,128,1]{1,0,2:T(8,128)}, u32[]{:S(2)}) copy-start(f32[256,128,1]{1,0,2:T(8,128)} %constant.30) | copy-start | bytes 393220
  55.1 18.2 %all-to-all-start.1 = ((f32[16,1,1,4,2,8,128]{6,5,4,3,2,1,0:T(8,128)}), f32[16,1,1,4,2,8,128]{6,5,4,3,2,1,0:T(8,128)S(1)}, u32[]{:S(2)}, u32[]{:S(2)}) async-start(f32[16,1,1,4,2,8,128]{6,5,4,3,2,1,0:T(8,128)} %bitcast.119), calls=%async_computation.1 | async-start | bytes 1048576 | tf_op jit(solution)/shard_map/all_to_all | solution.py:405
  73.3 24.8 %all-to-all-start.5 = ((f32[16,1,1,4,2,8,128]{6,5,4,3,2,1,0:T(8,128)}), f32[16,1,1,4,2,8,128]{6,5,4,3,2,1,0:T(8,128)S(1)}, u32[]{:S(2)}, u32[]{:S(2)}) async-start(f32[16,1,1,4,2,8,128]{6,5,4,3,2,1,0:T(8,128)} %bitcast.117), calls=%async_computation.5 | async-start | bytes 1048576 | tf_op jit(solution)/shard_map/all_to_all | solution.py:405
  81.5 23.4 %copy-start.3 = (f32[256,128,1]{1,0,2:T(8,128)S(1)}, f32[256,128,1]{1,0,2:T(8,128)}, u32[]{:S(2)}) copy-start(f32[256,128,1]{1,0,2:T(8,128)} %constant.32) | copy-start | bytes 393220
  98.2 29.0 %all-to-all-start.2 = ((f32[16,1,8,8,128]{4,2,3,1,0:T(8,128)}), f32[16,1,8,8,128]{4,2,3,1,0:T(8,128)S(1)}, u32[]{:S(2)}, u32[]{:S(2)}) async-start(f32[16,1,8,8,128]{4,2,3,1,0:T(8,128)} %convolution_bitcast_fusion.6), calls=%async_computation.2 | async-start | bytes 1048576 | tf_op jit(solution)/shard_map/all_to_all | solution.py:397
  127.1 16.8 %all-to-all-start.6 = ((f32[16,1,8,8,128]{4,2,3,1,0:T(8,128)}), f32[16,1,8,8,128]{4,2,3,1,0:T(8,128)S(1)}, u32[]{:S(2)}, u32[]{:S(2)}) async-start(f32[16,1,8,8,128]{4,2,3,1,0:T(8,128)} %convolution_bitcast_fusion.2), calls=%async_computation.6 | async-start | bytes 1048576 | tf_op jit(solution)/shard_map/all_to_all | solution.py:397
  144.0 18.1 %all-to-all-start.3 = ((f32[16,1,1,4,2,8,128]{6,5,4,3,2,1,0:T(8,128)}), f32[16,1,1,4,2,8,128]{6,5,4,3,2,1,0:T(8,128)S(1)}, u32[]{:S(2)}, u32[]{:S(2)}) async-start(f32[16,1,1,4,2,8,128]{6,5,4,3,2,1,0:T(8,128)} %bitcast.118), calls=%async_computation.3 | async-start | bytes 1048576 | tf_op jit(solution)/shard_map/all_to_all | solution.py:405
  162.1 17.6 %all-to-all-start.7 = ((f32[16,1,1,4,2,8,128]{6,5,4,3,2,1,0:T(8,128)}), f32[16,1,1,4,2,8,128]{6,5,4,3,2,1,0:T(8,128)S(1)}, u32[]{:S(2)}, u32[]{:S(2)}) async-start(f32[16,1,1,4,2,8,128]{6,5,4,3,2,1,0:T(8,128)} %bitcast.116), calls=%async_computation.7 | async-start | bytes 1048576 | tf_op jit(solution)/shard_map/all_to_all | solution.py:405
  278.4 7.6 %copy-start.1 = (f32[1,8,256,128]{3,2,1,0:T(8,128)S(1)}, f32[1,8,256,128]{3,2,1,0:T(8,128)}, u32[]{:S(2)}) copy-start(f32[1,8,256,128]{3,2,1,0:T(8,128)} %param.16) | copy-start | bytes 3145732
  280.4 4.8 %copy-start.2 = (f32[1024,128]{1,0:T(8,128)S(1)}, f32[1024,128]{1,0:T(8,128)}, u32[]{:S(2)}) copy-start(f32[1024,128]{1,0:T(8,128)} %get-tuple-element.51) | copy-start | bytes 1572868

commit v2 on v1

--- a/solution.py
+++ b/solution.py
@@ -375,9 +375,406 @@
     )(*totals)
 
 
+def split_dot(high_low, value, turned=False):
+    hi = value.astype(jnp.bfloat16)
+    lo = (value - hi.astype(jnp.float32)).astype(jnp.bfloat16)
+    table_hi, table_lo = high_low
+    mul = t_mul if turned else lambda a, b: jnp.dot(a, b, preferred_element_type=jnp.float32)
+    return mul(table_hi, hi) + (mul(table_hi, lo) + mul(table_lo, hi))
+
+
+def halves(value):
+    hi = value.astype(jnp.bfloat16)
+    return hi, (value - hi.astype(jnp.float32)).astype(jnp.bfloat16)
+
+
+class Sizes:
+    def __init__(self, bands, lat_rows, lon, features, hidden):
+        self.bands, self.lat_rows, self.lon = bands, lat_rows, lon
+        self.features, self.hidden = features, hidden
+        self.lats = bands * lat_rows
+        self.waves = MW // bands
+        self.pairs = 2 * self.waves
+        self.block = self.pairs * lat_rows
+        self.rows = lat_rows * lon
+        self.all_pairs = 2 * MW
+
+
+class Exchange:
+    @staticmethod
+    def sems(size):
+        return [pltpu.SemaphoreType.DMA, pltpu.SemaphoreType.DMA((size.bands,))]
+
+    def __init__(self, size, out, got, ssem, rsem):
+        self.size, self.out, self.got, self.ssem, self.rsem = size, out, got, ssem, rsem
+        self.me = lax.axis_index("lat")
+
+    def part(self, ref, band, first, count):
+        return ref.at[pl.ds(pl.multiple_of(band * self.size.block + first, 8), count), :]
+
+    def start(self, first=0, count=None):
+        count = self.size.block if count is None else count
+
+        @pl.loop(1, self.size.bands)
+        def _(step):
+            to = lax.rem(self.me + step, self.size.bands)
+            send(self.part(self.out, to, first, count), self.part(self.got, self.me, first, count),
+                 self.ssem, self.rsem.at[step], {"lat": to})
+
+        self.part(self.got, self.me, first, count)[...] = self.part(self.out, self.me, first, count)[...]
+
+    def wait(self):
+        @pl.loop(1, self.size.bands)
+        def _(step):
+            wait_bytes(self.part(self.got, 0, 0, self.size.block), self.rsem.at[step])
+
+    def drain(self):
+        wait_bytes(self.out.at[pl.ds(0, (self.size.bands - 1) * self.size.block), :], self.ssem)
+
+
+def greet_lat(size, also=0):
+    me = lax.axis_index("lat")
+
+    @pl.loop(1, size.bands)
+    def _(step):
+        signal_to({"lat": lax.rem(me + step, size.bands)})
+
+
+def greeted(count):
+    pl.semaphore_wait(pltpu.get_barrier_semaphore(), count)
+
+
+def build_operator(size, table_ref, quad_ref, op_hi, op_lo):
+    quad = quad_ref[...]
+    for m in range(size.waves):
+        table = table_ref[m]
+        base = split_dot(halves(table), table, turned=True)
+        hi, lo = halves(base * quad)
+        op_hi[m] = hi
+        op_lo[m] = lo
+
+
+def legendre(size, op_hi, op_lo, got, out, turned):
+    for m in range(size.waves):
+        value = jnp.concatenate(
+            [got[pl.ds(2 * m + p, size.lats, stride=size.pairs), :] for p in (0, 1)], axis=1)
+        back = split_dot((op_hi[m], op_lo[m]), value, turned)
+        for p in (0, 1):
+            for d in range(size.bands):
+                out[pl.ds(d * size.block + (2 * m + p) * size.lat_rows, size.lat_rows), :] = (
+                    back[d * size.lat_rows:(d + 1) * size.lat_rows, p * LANES:(p + 1) * LANES])
+
+
+def analyse(size, high_low, first, second, lat, out):
+    wav = split_dot(high_low, jnp.concatenate([first, second], axis=1))
+    for u in (0, 1):
+        for d in range(size.bands):
+            out[pl.ds(pl.multiple_of(d * size.block + (lat + u) * size.pairs, 8), size.pairs), :] = (
+                wav[d * size.pairs:(d + 1) * size.pairs, u * LANES:(u + 1) * LANES])
+
+
+def synthesise(size, high_low, got, put):
+    for lat in range(0, size.lat_rows, 2):
+        value = jnp.concatenate(
+            [got[pl.ds(lat + u, size.all_pairs, stride=size.lat_rows), :] for u in (0, 1)], axis=1)
+        out = split_dot(high_low, value)
+        for u in (0, 1):
+            put(lat + u, out[:, u * LANES:(u + 1) * LANES])
+
+
+def forward_tile(size, row, x, w1, w2, w3, keep):
+    h1t, s1_ref, h2t, s2_ref, xt = keep
+    rows = x.astype(jnp.bfloat16)
+    span = pl.ds(row, size.lon)
+    if xt is not None:
+        xt[:, span] = rows.T
+    h1, s1 = silu_pair(jnp.dot(rows, w1[...], preferred_element_type=jnp.float32))
+    h1 = h1.astype(jnp.bfloat16)
+    s1_ref[span, :] = s1.astype(jnp.bfloat16)
+    h1t[:, span] = h1.T
+    h2, s2 = silu_pair(jnp.dot(h1, w2[...], preferred_element_type=jnp.float32))
+    h2 = h2.astype(jnp.bfloat16)
+    s2_ref[span, :] = s2.astype(jnp.bfloat16)
+    h2t[:, span] = h2.T
+    return x + tend_weight * jnp.dot(h2, w3[...], preferred_element_type=jnp.float32)
+
+
+def table_copy(size, table_hbm, table_ref, sem):
+    waves = size.waves
+    return pltpu.make_async_copy(table_hbm.at[pl.ds(lax.axis_index("lat") * waves, waves)], table_ref, sem)
+
+
+def first_kernel(size, x_ref, c_ref, w1, w2, w3, table_hbm, quad, ana_hi, ana_lo, syt_hi, syt_lo, syn_hi, syn_lo,
+                 q_ref, backc_ref, h1t_hbm, s1_hbm, h2t_hbm, s2_hbm,
+                 table, op_hi, op_lo, h1t, s1, h2t, s2, outc, gotc, outm, gotm, backm, got2m,
+                 tsem, ksems, *sems):
+    xc = Exchange(size, outc, gotc, *sems[0:2])
+    xm = Exchange(size, outm, gotm, *sems[2:4])
+    x2 = Exchange(size, backm, got2m, *sems[4:6])
+    greet_lat(size)
+    table_in = table_copy(size, table_hbm, table, tsem)
+    table_in.start()
+
+    @pl.loop(0, size.lat_rows // 2)
+    def _(i):
+        analyse(size, (syt_hi[...], syt_lo[...]), c_ref[2 * i], c_ref[2 * i + 1], 2 * i, outc)
+
+    greeted(size.bands - 1)
+    xc.start()
+    table_in.wait()
+    build_operator(size, table, quad, op_hi, op_lo)
+    keeps = ((h1t, h1t_hbm, 1), (s1, s1_hbm, 0), (h2t, h2t_hbm, 1), (s2, s2_hbm, 0))
+
+    def keep_copies(i):
+        span = pl.ds(pl.multiple_of(i * 2 * size.lon, 2 * size.lon), 2 * size.lon)
+        for k, (src, dst, axis) in enumerate(keeps):
+            where = (slice(None), span) if axis else (span, slice(None))
+            pltpu.make_async_copy(src.at[where], dst.at[where], ksems.at[k]).start()
+
+    @pl.loop(0, size.lat_rows // 2)
+    def _(i):
+        moved = [
+            forward_tile(size, pl.multiple_of((2 * i + u) * size.lon, size.lon), x_ref[2 * i + u],
+                         w1, w2, w3, (h1t, s1, h2t, s2, None))
+            for u in (0, 1)
+        ]
+        analyse(size, (ana_hi[...], ana_lo[...]), moved[0], moved[1], 2 * i, outm)
+        xm.start(pl.multiple_of(2 * i * size.pairs, 2 * size.pairs), 2 * size.pairs)
+        keep_copies(i)
+
+    xc.wait()
+    legendre(size, op_hi, op_lo, gotc, backc_ref, True)
+    xm.wait()
+    legendre(size, op_hi, op_lo, gotm, backm, False)
+    x2.start()
+    x2.wait()
+
+    def put(lat, value):
+        q_ref[lat] = value
+
+    synthesise(size, (syn_hi[...], syn_lo[...]), got2m, put)
+    for x in (xc, xm, x2):
+        x.drain()
+    for k, (src, dst, _) in enumerate(keeps):
+        pltpu.make_async_copy(src, dst, ksems.at[k]).wait()
+
+
+def weight_gradients(size, h1t, h2t, xt, gt, ga1, ga2, put):
+    blocks = size.hidden // LANES
+    dot = lambda a, b: jnp.dot(a, b, preferred_element_type=jnp.float32)
+    half = size.hidden // 2
+    for top in (0, half):
+        put(blocks * CHUNK + top, dot(h2t[pl.ds(top, half), :], gt[...]))
+
+    @pl.loop(0, blocks // 2)
+    def _(i):
+        columns = pl.ds(pl.multiple_of(i * 2 * LANES, 2 * LANES), 2 * LANES)
+        for top in (0, half):
+            part = dot(h1t[pl.ds(top, half), :], ga2[:, columns])
+            for u in (0, 1):
+                put(pl.multiple_of((2 * i + u) * CHUNK + top, half), part[:, u * LANES:(u + 1) * LANES])
+        part = dot(xt[...], ga1[:, columns])
+        for u in (0, 1):
+            put(pl.multiple_of((blocks + 1) * CHUNK + (2 * i + u) * LANES, LANES),
+                part[:, u * LANES:(u + 1) * LANES])
+
+
+def middle_kernel(size, q_ref, backc_ref, w1, w2, w3, table_hbm, quad,
+                  ana_hi, ana_lo, syt_hi, syt_lo, ant_hi, ant_lo,
+                  p_ref, backm_ref, g_hbm,
+                  table, op_hi, op_lo, h1t, s1, h2t, s2, xt, pulled, gt, ga1, ga2, g,
+                  got2c, outm, gotm, outg, gotg, backg, got2g, tsem, gsem, *sems):
+    x2c = Exchange(size, backc_ref, got2c, *sems[0:2])
+    xm = Exchange(size, outm, gotm, *sems[2:4])
+    xg = Exchange(size, outg, gotg, *sems[4:6])
+    x2g = Exchange(size, backg, got2g, *sems[6:8])
+    greet_lat(size)
+    table_in = table_copy(size, table_hbm, table, tsem)
+    table_in.start()
+    greeted(size.bands - 1)
+    x2c.start()
+    table_in.wait()
+    build_operator(size, table, quad, op_hi, op_lo)
+
+    @pl.loop(0, size.lat_rows // 2)
+    def _(i):
+        moved = [
+            forward_tile(size, pl.multiple_of((2 * i + u) * size.lon, size.lon), q_ref[2 * i + u],
+                         w1, w2, w3, (h1t, s1, h2t, s2, xt))
+            for u in (0, 1)
+        ]
+        analyse(size, (ana_hi[...], ana_lo[...]), moved[0], moved[1], 2 * i, outm)
+
+    x2c.wait()
+
+    def put(lat, value):
+        pulled[lat] = value
+
+    synthesise(size, (ant_hi[...], ant_lo[...]), got2c, put)
+    xm.start()
+
+    @pl.loop(0, size.lat_rows // 2)
+    def _(i):
+        span = pl.ds(pl.multiple_of(2 * i * size.lon, 2 * size.lon), 2 * size.lon)
+        p = jnp.concatenate([pulled[2 * i], pulled[2 * i + 1]], axis=0)
+        g_t = (tend_weight * p).astype(jnp.bfloat16)
+        gt[span, :] = g_t
+        g_a2 = (mul_t(g_t, w3[...]) * s2[span, :].astype(jnp.float32)).astype(jnp.bfloat16)
+        ga2[span, :] = g_a2
+        g_a1 = (mul_t(g_a2, w2[...]) * s1[span, :].astype(jnp.float32)).astype(jnp.bfloat16)
+        ga1[span, :] = g_a1
+        grad = p + mul_t(g_a1, w1[...])
+        analyse(size, (syt_hi[...], syt_lo[...]), grad[:size.lon], grad[size.lon:], 2 * i, outg)
+        xg.start(pl.multiple_of(2 * i * size.pairs, 2 * size.pairs), 2 * size.pairs)
+
+    def keep(row, value):
+        g[pl.ds(row, value.shape[0]), :] = value
+
+    weight_gradients(size, h1t, h2t, xt, gt, ga1, ga2, keep)
+    xm.wait()
+    legendre(size, op_hi, op_lo, gotm, backm_ref, False)
+    g_out = pltpu.make_async_copy(g, g_hbm, gsem)
+    g_out.start()
+    xg.wait()
+    legendre(size, op_hi, op_lo, gotg, backg, True)
+    x2g.start()
+    x2g.wait()
+
+    def put_pulled(lat, value):
+        p_ref[lat] = value
+
+    synthesise(size, (ant_hi[...], ant_lo[...]), got2g, put_pulled)
+    for x in (x2c, xm, xg, x2g):
+        x.drain()
+    g_out.wait()
+
+
+def last_kernel(size, p_ref, x_ref, backm_ref, w2, w3, syn_hi, syn_lo, g_hbm, h1t_hbm, s1_hbm, h2t_hbm, s2_hbm,
+                final_ref, o_ref, h1t, s1, h2t, s2, xt, gt, ga1, ga2, got2m, lsems, ssem, rsem, *scratch):
+    place = Place(size.bands)
+    chunks = size.hidden // LANES + 2
+    red = Reduce(place, chunks, (scratch[0], o_ref, *scratch[1:]))
+    g = red.g
+    x2m = Exchange(size, backm_ref, got2m, ssem, rsem)
+    greet_lat(size)
+    signal_to(place.across_core)
+    loads = [pltpu.make_async_copy(src, dst, lsems.at[k]) for k, (src, dst) in enumerate(
+        ((s2_hbm, s2), (h2t_hbm, h2t), (h1t_hbm, h1t), (g_hbm, g), (s1_hbm, s1)))]
+    for load in loads:
+        load.start()
+    greeted(size.bands)
+    x2m.start()
+    loads[0].wait()
+
+    tiles = size.lat_rows // 2
+
+    def span_of(i):
+        return pl.ds(pl.multiple_of(2 * i * size.lon, 2 * size.lon), 2 * size.lon)
+
+    @pl.loop(0, tiles)
+    def _(i):
+        span = span_of(i)
+        xt[:, span] = jnp.concatenate([x_ref[2 * i], x_ref[2 * i + 1]], axis=0).astype(jnp.bfloat16).T
+        g_t = (tend_weight * jnp.concatenate([p_ref[2 * i], p_ref[2 * i + 1]], axis=0)).astype(jnp.bfloat16)
+        gt[span, :] = g_t
+        ga2[span, :] = (mul_t(g_t, w3[...]) * s2[span, :].astype(jnp.float32)).astype(jnp.bfloat16)
+
+    for load in loads[1:]:
+        load.wait()
+
+    @pl.loop(0, tiles)
+    def _(i):
+        span = span_of(i)
+        ga1[span, :] = (mul_t(ga2[span, :], w2[...]) * s1[span, :].astype(jnp.float32)).astype(jnp.bfloat16)
+
+    def put(row, value):
+        g[pl.ds(row, value.shape[0]), :] += value
+
+    weight_gradients(size, h1t, h2t, xt, gt, ga1, ga2, put)
+
+    @pl.loop(0, red.steps)
+    def _(t):
+        red.step(t)
+
+    x2m.wait()
+
+    def put_final(lat, value):
+        final_ref[lat] = value
+
+    synthesise(size, (syn_hi[...], syn_lo[...]), got2m, put_final)
+    x2m.drain()
+    red.drain()
+
+
+def fused_body(size, state, cotangent, w1, w2, w3):
+    analysis, synthesis = grid_tables(size.lon, MW)
+    table, quad = legendre_tables(size.lats, MW)
+    pair = lambda t: [jnp.asarray(part) for part in np_halves(t)]
+    ana_t, syn_t = pair(analysis.T), pair(synthesis.T)
+    ana, syn = pair(analysis), pair(synthesis)
+    table, quad = jnp.asarray(table), jnp.asarray(quad)[None, :]
+    vmem = pl.BlockSpec(memory_space=pltpu.VMEM)
+    hbm = pl.BlockSpec(memory_space=pl.ANY)
+    f32, bf16 = jnp.float32, jnp.bfloat16
+    field = jax.ShapeDtypeStruct(state.shape[1:], f32)
+    blocks = jax.ShapeDtypeStruct((size.bands * size.block, LANES), f32)
+    wide = jax.ShapeDtypeStruct((size.rows, size.hidden), bf16)
+    tall = jax.ShapeDtypeStruct((size.hidden, size.rows), bf16)
+    grads = jax.ShapeDtypeStruct(((size.hidden // LANES + 2) * CHUNK, LANES), f32)
+    buf = lambda shape: pltpu.VMEM(shape.shape, shape.dtype)
+    dma = pltpu.SemaphoreType.DMA
+    operator = [pltpu.VMEM((size.waves, MW, size.lats), f32)] + [
+        pltpu.VMEM((size.waves, size.lats, size.lats), bf16)] * 2
+    narrow = pltpu.VMEM((size.rows, LANES), bf16)
+    x_t = pltpu.VMEM((LANES, size.rows), bf16)
+    work = size.rows * size.hidden * (size.hidden + 2 * size.features)
+    call = lambda kernel, ident, flops, ins, outs, shapes, scratch: pl.pallas_call(
+        functools.partial(kernel, size), in_specs=ins, out_specs=outs, out_shape=shapes, scratch_shapes=scratch,
+        cost_estimate=pl.CostEstimate(flops=flops, bytes_accessed=2**24, transcendentals=0),
+        compiler_params=pltpu.CompilerParams(
+            collective_id=ident, has_side_effects=True, vmem_limit_bytes=60 * 2**20))
+    x0 = state[0]
+    q1, back_c, *saved = call(
+        first_kernel, 1, 2 * work, [vmem] * 5 + [hbm] + [vmem] * 7, [vmem] * 2 + [hbm] * 4,
+        [field, blocks, tall, wide, tall, wide],
+        operator + [buf(tall), buf(wide), buf(tall), buf(wide)] + [buf(blocks)] * 6
+        + [dma, dma((4,))] + Exchange.sems(size) * 3,
+    )(x0, cotangent[0], w1, w2, w3, table, quad, *ana_t, *syn_t, *syn)
+    pulled0, back_m, sums = call(
+        middle_kernel, 2, 6 * work, [vmem] * 5 + [hbm] + [vmem] * 7, [vmem, vmem, hbm],
+        [field, blocks, grads],
+        operator + [buf(tall), buf(wide), buf(tall), buf(wide), x_t, buf(field), narrow, buf(wide), buf(wide),
+                    buf(grads)]
+        + [buf(blocks)] * 7 + [dma, dma] + Exchange.sems(size) * 4,
+    )(q1, back_c, w1, w2, w3, table, quad, *ana_t, *syn_t, *ana)
+    reduce_scratch = Reduce.scratch(size.hidden // LANES + 2, size.bands // 4)
+    final, totals = call(
+        last_kernel, 3, 4 * work, [vmem] * 7 + [hbm] * 5, [vmem, vmem], [field, grads],
+        [buf(tall), buf(wide), buf(tall), buf(wide), x_t, narrow, buf(wide), buf(wide), buf(blocks), dma((5,))]
+        + Exchange.sems(size) + reduce_scratch[:1] + reduce_scratch[2:],
+    )(pulled0, x0, back_m, w2, w3, *syn, sums, *saved)
+    lanes = size.hidden // LANES
+    middle, last, first = totals[:lanes * CHUNK], totals[lanes * CHUNK:(lanes + 1) * CHUNK], totals[(lanes + 1) * CHUNK:]
+    unblock = lambda t, rows: t.reshape(lanes, rows, LANES).transpose(1, 0, 2).reshape(rows, size.hidden)
+    return final[None], unblock(first, size.features), unblock(middle, size.hidden), last
+
+
+def np_halves(table):
+    hi = table.astype(jnp.bfloat16)
+    return hi, (table - hi.astype(np.float32)).astype(jnp.bfloat16)
+
+
+def fits_fused(size, sample):
+    return (sample == 1 and size.lat_rows == 8 and size.pairs == 8 and size.lon % 256 == 0
+            and size.lats % LANES == 0 and size.bands % 8 == 0)
+
+
 def body(state, cotangent, w1, w2, w3):
     sample, lat_rows, lon_count, features = state.shape
     bands = lax.axis_size("lat")
+    size = Sizes(bands, lat_rows, lon_count, features, w1.shape[1])
+    if fits_fused(size, sample) and fits_reduce(bands, lax.axis_size("dp"), features, w1.shape[1]):
+        return fused_body(size, state, cotangent, w1, w2, w3)
     lat_count = lat_rows * bands
     waves = MW // bands
     analysis, synthesis = grid_tables(lon_count, MW)

time: 287 us -> 206 us (0.72)
  waiting for transfers between devices: 58.8 us -> 0 us
  Pallas kernels: 144 us -> 197 us
  starting transfers between devices: 52.3 us -> 0 us
  matrix products: 18.2 us -> 0 us
  local copies, waits for them, and re-layouts: 12.1 us -> 8.94 us
    all_to_all x8 -> x0, waiting for transfers between devices: 58.8 us -> none  [the longest x4 29.5 us: spectral(): back = lax.all_to_all(back, 'lat', split_axis=0, concat_axis=0, tiled=True)]
    pallas_call x5 -> x3, Pallas kernels: 144 us -> 197 us  [the longest x1 99.2 us: fused_body(): call(last_kernel, 3, 4 * work, [vmem] * 7 + [hbm] * 5, [vmem, vmem], [fie...]
    all_to_all x8 -> x0, starting transfers between devices: 52.3 us -> none  [the longest x4 26.3 us: spectral(): back = lax.all_to_all(back, 'lat', split_axis=0, concat_axis=0, tiled=True)]
    dot_general x13 -> x0, matrix products: 18.2 us -> none  [the longest x4 8.53 us: spectral(): wav = jnp.einsum('bjxf,xq->bqjf', field, first, precision=high)]
    unnamed x19 -> x3, local copies, waits for them, and re-layouts: 7.66 us -> 0.97 us
    slice x0 -> x2, local copies, waits for them, and re-layouts: none -> 4.52 us  [the longest x1 2.46 us: fused_body(): totals[:lanes * CHUNK]]
  transfers between devices with their start and end apart: 8 -> 0, of which waited for: 6 -> 0; matrix products, arithmetic and copies ran while one was open for 6% -> 0% of each run, Pallas kernels for 11% -> 0%
where the time goes in v2:
time: 206 us
  Pallas kernels  197 us (96%)
  local copies, waits for them, and re-layouts  8.94 us (4%)
    pallas_call x1, Pallas kernels, fused_body(): call(last_kernel, 3, 4 * work, [vmem] * 7 + [hbm] * 5, [vmem, vmem], [fie...  99.2 us
    pallas_call x1, Pallas kernels, fused_body(): call(middle_kernel, 2, 6 * work, [vmem] * 5 + [hbm] + [vmem] * 7, [vmem,...  56.6 us
    pallas_call x1, Pallas kernels, fused_body(): call(first_kernel, 1, 2 * work, [vmem] * 5 + [hbm] + [vmem] * 7, [vmem] *...  40.9 us

profile of v2, /device:TPU:1, one launch (start us, length us, event | category | flops | bytes accessed | tf_op | source)
XLA Modules:
  0.0 206.3 jit_solution(14329745078380842417)
XLA Ops:
  0.6 40.9 %shard_map.174 = (f32[8,256,128]{2,1,0:T(8,128)}, f32[1024,128]{1,0:T(8,128)}, bf16[1024,2048]{1,0:T(8,128)(2,1)}, bf16[2048,1024]{1,0:T(8,128)(2,1)}, bf16[1024...) custom-call(f32[8,256,128]{2,1,0:T(8,128)} %bitcast.23, f32[8,256,128]{2,1,0:T(8,128)} %bitcast.22, bf16[128,1024]{1,0:T(8,128)(2,1)} %w1.3, ...), custom_call_target="tpu_custom_call" | custom-call | flops 5368709120 | bytes 16777216 | tf_op jit(solution)/shard_map/pallas_call | solution.py:737
  41.5 56.6 %shard_map.175 = (f32[8,256,128]{2,1,0:T(8,128)}, f32[1024,128]{1,0:T(8,128)}, f32[10240,128]{1,0:T(8,128)}) custom-call(f32[8,256,128]{2,1,0:T(8,128)} %get-tuple-element.15.q_ref, f32[1024,128]{1,0:T(8,128)} %get-tuple-element.16.backc_ref, bf16[128,1024]{1,0:T(8,128)(2,1)} %w1.3, bf16[1024,1024]{1,0:T(8,128)(2,1)} %w2.5, bf16[1024,128]{1,0:T(8,128)(2,1)} %w3.5, ...), custom_call_target="tpu_custom_call" | custom-call | flops 16106127360 | bytes 16777216 | tf_op jit(solution)/shard_map/pallas_call | solution.py:743
  98.1 99.2 %shard_map.176 = (f32[8,256,128]{2,1,0:T(8,128)}, f32[10240,128]{1,0:T(8,128)}) custom-call(f32[8,256,128]{2,1,0:T(8,128)} %get-tuple-element.17.p_ref, f32[8,256,128]{2,1,0:T(8,128)} %bitcast.24, f32[1024,128]{1,0:T(8,128)} %get-tuple-element.18.backm_ref, bf16[1024,1024]{1,0:T(8,128)(2,1)} %w2.5, bf16[1024,128]{1,0:T(8,128)(2,1)} %w3.5, ...), custom_call_target="tpu_custom_call" | custom-call | flops 10737418240 | bytes 16777216 | tf_op jit(solution)/shard_map/pallas_call | solution.py:751
  197.3 2.1 fusion
  199.4 2.5 %slice.10 = f32[8192,128]{1,0:T(8,128)S(1)} slice(f32[10240,128]{1,0:T(8,128)} %get-tuple-element.25), slice={[0:8192], [0:128]} | slice | bytes 8388608 | tf_op jit(solution)/shard_map/slice | solution.py:757
  201.8 0.0 copy-start
  201.8 2.6 %copy.25 = f32[8,128,8,128]{3,2,0,1:T(8,128)} copy(f32[8,128,8,128]{3,2,1,0:T(8,128)S(1)} %bitcast.17) | data formatting | bytes 8388608 | tf_op jit(solution)/shard_map/reshape | solution.py:758
  204.4 0.8 copy.26
  205.3 0.0 copy-done
  205.3 1.0 copy.28
Async XLA Ops:
  201.8 3.5 %copy-start = (f32[8,256,128]{2,1,0:T(8,128)S(1)}, f32[8,256,128]{2,1,0:T(8,128)}, u32[]{:S(2)}) copy-start(f32[8,256,128]{2,1,0:T(8,128)} %get-tuple-element.24) | copy-start | bytes 3145732

commit v3 on v2

--- a/solution.py
+++ b/solution.py
@@ -162,6 +162,9 @@
 MESH_ID = pl.DeviceIdType.MESH
 LANES = 128
 CHUNK = 1024
+SPAN = CHUNK
+HALF = SPAN // 2
+LAGS = (0, 1, 3, 5, 7, 9, 11, 13, 14)
 
 
 class Place:
@@ -209,11 +212,11 @@
 
     @staticmethod
     def scratch(chunks, depth):
-        rows = lambda count: pltpu.VMEM((chunks * count, LANES), jnp.float32)
+        rows = lambda parts: pltpu.VMEM((chunks * SPAN // parts, LANES), jnp.float32)
         sems = lambda *dims: pltpu.SemaphoreType.DMA((chunks,) + dims)
         return [
-            rows(CHUNK), rows(CHUNK), rows(512), rows(256), rows(128),
-            pltpu.VMEM((chunks, depth - 1, 256 // depth // 2, LANES), jnp.float32),
+            rows(1), rows(1), rows(2), rows(4), rows(8),
+            pltpu.VMEM((chunks, depth - 1, SPAN // 8 // depth, LANES), jnp.float32),
             sems(), sems(2), sems(2), sems(depth - 1), sems(depth - 1), sems(2), sems(2), sems(),
             pltpu.SemaphoreType.DMA((Reduce.SENDS,)),
         ]
@@ -222,48 +225,48 @@
         (self.g, self.o, self.r0, self.r1, self.r2, self.r3,
          self.d0, self.m1, self.m2, self.z3, self.z4, self.m5, self.m6, self.d7, self.sent) = refs
         self.place, self.chunks = place, chunks
-        self.piece = 64 // place.depth
+        self.piece = SPAN // 16 // place.depth
         p = place
-        half = p.core * 512
+        half = p.core * HALF
         self.first = ((p.across_x, p.x), (p.across_y, p.y))
         self.second = (self.first[1], self.first[0])
-        self.quarter = (half, half + 256)
-        self.eighth = tuple(self.quarter[i] + self.first[i][1] * 128 for i in (0, 1))
-        self.sixteenth = tuple(self.eighth[i] + self.second[i][1] * 64 for i in (0, 1))
+        self.quarter = (half, half + HALF // 2)
+        self.eighth = tuple(self.quarter[i] + self.first[i][1] * (HALF // 4) for i in (0, 1))
+        self.sixteenth = tuple(self.eighth[i] + self.second[i][1] * (HALF // 8) for i in (0, 1))
         self.own = tuple(self.sixteenth[i] + p.z * self.piece for i in (0, 1))
 
-    def rows(self, ref, k, offset, count, span=CHUNK):
+    def rows(self, ref, k, offset, count, span=SPAN):
         return ref.at[pl.ds(pl.multiple_of(k * span + offset, 8), count), :]
 
     def stage0(self, k):
-        other = (1 - self.place.core) * 512
-        send(self.rows(self.g, k, other, 512), self.rows(self.r0, k, 0, 512, 512),
+        other = (1 - self.place.core) * HALF
+        send(self.rows(self.g, k, other, HALF), self.rows(self.r0, k, 0, HALF, HALF),
              self.sent.at[0], self.d0.at[k], self.place.across_core)
 
     def stage1(self, k):
-        wait_bytes(self.rows(self.r0, k, 0, 512, 512), self.d0.at[k])
-        mine = self.rows(self.g, k, self.place.core * 512, 512)
-        mine[...] += self.rows(self.r0, k, 0, 512, 512)[...]
+        wait_bytes(self.rows(self.r0, k, 0, HALF, HALF), self.d0.at[k])
+        mine = self.rows(self.g, k, self.place.core * HALF, HALF)
+        mine[...] += self.rows(self.r0, k, 0, HALF, HALF)[...]
         for i in (0, 1):
             device, bit = self.first[i]
-            send(self.rows(self.g, k, self.quarter[i] + (1 - bit) * 128, 128),
-                 self.rows(self.r1, k, i * 128, 128, 256), self.sent.at[1], self.m1.at[k, i], device)
+            send(self.rows(self.g, k, self.quarter[i] + (1 - bit) * (HALF // 4), HALF // 4),
+                 self.rows(self.r1, k, i * (HALF // 4), HALF // 4, HALF // 2), self.sent.at[1], self.m1.at[k, i], device)
 
     def stage2(self, k):
         for i in (0, 1):
-            got = self.rows(self.r1, k, i * 128, 128, 256)
+            got = self.rows(self.r1, k, i * (HALF // 4), HALF // 4, HALF // 2)
             wait_bytes(got, self.m1.at[k, i])
-            self.rows(self.g, k, self.eighth[i], 128)[...] += got[...]
+            self.rows(self.g, k, self.eighth[i], HALF // 4)[...] += got[...]
         for i in (0, 1):
             device, bit = self.second[i]
-            send(self.rows(self.g, k, self.eighth[i] + (1 - bit) * 64, 64),
-                 self.rows(self.r2, k, i * 64, 64, 128), self.sent.at[2], self.m2.at[k, i], device)
+            send(self.rows(self.g, k, self.eighth[i] + (1 - bit) * (HALF // 8), HALF // 8),
+                 self.rows(self.r2, k, i * (HALF // 8), HALF // 8, HALF // 4), self.sent.at[2], self.m2.at[k, i], device)
 
     def stage3(self, k):
         for i in (0, 1):
-            got = self.rows(self.r2, k, i * 64, 64, 128)
+            got = self.rows(self.r2, k, i * (HALF // 8), HALF // 8, HALF // 4)
             wait_bytes(got, self.m2.at[k, i])
-            self.rows(self.g, k, self.sixteenth[i], 64)[...] += got[...]
+            self.rows(self.g, k, self.sixteenth[i], HALF // 8)[...] += got[...]
         for step in range(1, self.place.depth):
             layer, device = self.place.along_z(step)
             for i in (0, 1):
@@ -289,41 +292,41 @@
         for step in range(1, self.place.depth):
             wait_bytes(self.r3.at[k, step - 1], self.z4.at[k, step - 1])
         for i in (0, 1):
-            mine = self.rows(self.o, k, self.sixteenth[i], 64)
+            mine = self.rows(self.o, k, self.sixteenth[i], HALF // 8)
             send(mine, mine, self.sent.at[5], self.m5.at[k, i], self.second[i][0])
 
     def stage6(self, k):
         for i in (0, 1):
-            wait_bytes(self.rows(self.r2, k, 0, 64, 128), self.m5.at[k, i])
+            wait_bytes(self.rows(self.r2, k, 0, HALF // 8, HALF // 4), self.m5.at[k, i])
         for i in (0, 1):
-            mine = self.rows(self.o, k, self.eighth[i], 128)
+            mine = self.rows(self.o, k, self.eighth[i], HALF // 4)
             send(mine, mine, self.sent.at[6], self.m6.at[k, i], self.first[i][0])
 
     def stage7(self, k):
         for i in (0, 1):
-            wait_bytes(self.rows(self.r1, k, 0, 128, 256), self.m6.at[k, i])
-        mine = self.rows(self.o, k, self.place.core * 512, 512)
+            wait_bytes(self.rows(self.r1, k, 0, HALF // 4, HALF // 2), self.m6.at[k, i])
+        mine = self.rows(self.o, k, self.place.core * HALF, HALF)
         send(mine, mine, self.sent.at[7], self.d7.at[k], self.place.across_core)
 
     def stage8(self, k):
-        wait_bytes(self.rows(self.r0, k, 0, 512, 512), self.d7.at[k])
+        wait_bytes(self.rows(self.r0, k, 0, HALF, HALF), self.d7.at[k])
 
     def step(self, t):
         stages = [self.stage0, self.stage1, self.stage2, self.stage3, self.stage4,
                   self.stage5, self.stage6, self.stage7, self.stage8]
-        for lag in range(8, -1, -1):
+        for stage, lag in reversed(list(zip(stages, LAGS))):
             k = t - lag
 
             @pl.when(jnp.logical_and(k >= 0, k < self.chunks))
-            def _(k=k, lag=lag):
-                stages[lag](k)
+            def _(k=k, stage=stage):
+                stage(k)
 
     @property
     def steps(self):
-        return self.chunks + 8
+        return self.chunks + LAGS[-1]
 
     def drain(self):
-        counts = [512, 256, 128, 2 * self.piece * (self.place.depth - 1)]
+        counts = [HALF, HALF // 2, HALF // 4, 2 * self.piece * (self.place.depth - 1)]
         counts = counts + counts[::-1]
         for i, count in enumerate(counts):
             wait_bytes(self.g.at[pl.ds(0, count * self.chunks), :], self.sent.at[i])
@@ -559,24 +562,41 @@
         pltpu.make_async_copy(src, dst, ksems.at[k]).wait()
 
 
-def weight_gradients(size, h1t, h2t, xt, gt, ga1, ga2, put):
-    blocks = size.hidden // LANES
-    dot = lambda a, b: jnp.dot(a, b, preferred_element_type=jnp.float32)
+def plain_dot(a, b):
+    return jnp.dot(a, b, preferred_element_type=jnp.float32)
+
+
+def last_gradient(size, h2t, gt, put):
     half = size.hidden // 2
     for top in (0, half):
-        put(blocks * CHUNK + top, dot(h2t[pl.ds(top, half), :], gt[...]))
-
-    @pl.loop(0, blocks // 2)
+        put(size.hidden // LANES * CHUNK + top, plain_dot(h2t[pl.ds(top, half), :], gt[...]))
+
+
+def middle_gradient(size, h1t, ga2, i, put):
+    half = size.hidden // 2
+    columns = pl.ds(pl.multiple_of(i * 2 * LANES, 2 * LANES), 2 * LANES)
+    for top in (0, half):
+        part = plain_dot(h1t[pl.ds(top, half), :], ga2[:, columns])
+        for u in (0, 1):
+            put(pl.multiple_of((2 * i + u) * CHUNK + top, half), part[:, u * LANES:(u + 1) * LANES])
+
+
+def first_gradient(size, xt, ga1, put):
+    blocks = size.hidden // LANES
+    for i in range(blocks // 2):
+        part = plain_dot(xt[...], ga1[:, pl.ds(i * 2 * LANES, 2 * LANES)])
+        for u in (0, 1):
+            put((blocks + 1) * CHUNK + (2 * i + u) * LANES, part[:, u * LANES:(u + 1) * LANES])
+
+
+def weight_gradients(size, h1t, h2t, xt, gt, ga1, ga2, put):
+    last_gradient(size, h2t, gt, put)
+
+    @pl.loop(0, size.hidden // LANES // 2)
     def _(i):
-        columns = pl.ds(pl.multiple_of(i * 2 * LANES, 2 * LANES), 2 * LANES)
-        for top in (0, half):
-            part = dot(h1t[pl.ds(top, half), :], ga2[:, columns])
-            for u in (0, 1):
-                put(pl.multiple_of((2 * i + u) * CHUNK + top, half), part[:, u * LANES:(u + 1) * LANES])
-        part = dot(xt[...], ga1[:, columns])
-        for u in (0, 1):
-            put(pl.multiple_of((blocks + 1) * CHUNK + (2 * i + u) * LANES, LANES),
-                part[:, u * LANES:(u + 1) * LANES])
+        middle_gradient(size, h1t, ga2, i, put)
+
+    first_gradient(size, xt, ga1, put)
 
 
 def middle_kernel(size, q_ref, backc_ref, w1, w2, w3, table_hbm, quad,
@@ -650,31 +670,29 @@
 
 
 def last_kernel(size, p_ref, x_ref, backm_ref, w2, w3, syn_hi, syn_lo, g_hbm, h1t_hbm, s1_hbm, h2t_hbm, s2_hbm,
-                final_ref, o_ref, h1t, s1, h2t, s2, xt, gt, ga1, ga2, got2m, lsems, ssem, rsem, *scratch):
+                final_ref, o_hbm, h1t, s1, h2t, s2, xt, gt, ga1, ga2, got2m, lsems, osem, ssem, rsem, *scratch):
     place = Place(size.bands)
-    chunks = size.hidden // LANES + 2
-    red = Reduce(place, chunks, (scratch[0], o_ref, *scratch[1:]))
+    blocks = size.hidden // LANES
+    tiles = size.lat_rows // 2
+    red = Reduce(place, blocks + 2, scratch)
     g = red.g
     x2m = Exchange(size, backm_ref, got2m, ssem, rsem)
     greet_lat(size)
     signal_to(place.across_core)
     loads = [pltpu.make_async_copy(src, dst, lsems.at[k]) for k, (src, dst) in enumerate(
-        ((s2_hbm, s2), (h2t_hbm, h2t), (h1t_hbm, h1t), (g_hbm, g), (s1_hbm, s1)))]
+        ((s2_hbm, s2), (g_hbm, g), (h1t_hbm, h1t), (h2t_hbm, h2t), (s1_hbm, s1)))]
     for load in loads:
         load.start()
     greeted(size.bands)
     x2m.start()
     loads[0].wait()
 
-    tiles = size.lat_rows // 2
-
     def span_of(i):
         return pl.ds(pl.multiple_of(2 * i * size.lon, 2 * size.lon), 2 * size.lon)
 
     @pl.loop(0, tiles)
     def _(i):
         span = span_of(i)
-        xt[:, span] = jnp.concatenate([x_ref[2 * i], x_ref[2 * i + 1]], axis=0).astype(jnp.bfloat16).T
         g_t = (tend_weight * jnp.concatenate([p_ref[2 * i], p_ref[2 * i + 1]], axis=0)).astype(jnp.bfloat16)
         gt[span, :] = g_t
         ga2[span, :] = (mul_t(g_t, w3[...]) * s2[span, :].astype(jnp.float32)).astype(jnp.bfloat16)
@@ -682,28 +700,75 @@
     for load in loads[1:]:
         load.wait()
 
-    @pl.loop(0, tiles)
-    def _(i):
-        span = span_of(i)
-        ga1[span, :] = (mul_t(ga2[span, :], w2[...]) * s1[span, :].astype(jnp.float32)).astype(jnp.bfloat16)
-
     def put(row, value):
         g[pl.ds(row, value.shape[0]), :] += value
 
-    weight_gradients(size, h1t, h2t, xt, gt, ga1, ga2, put)
+    middle_gradient(size, h1t, ga2, 0, put)
 
     @pl.loop(0, red.steps)
     def _(t):
         red.step(t)
 
-    x2m.wait()
-
-    def put_final(lat, value):
-        final_ref[lat] = value
-
-    synthesise(size, (syn_hi[...], syn_lo[...]), got2m, put_final)
+        @pl.when(t >= LAGS[-1])
+        def _():
+            rows = pl.ds(pl.multiple_of((t - LAGS[-1]) * CHUNK, CHUNK), CHUNK)
+            pltpu.make_async_copy(red.o.at[rows, :], o_hbm.at[rows, :], osem).start()
+
+        @pl.when(jnp.logical_and(lax.rem(t, 2) == 0, t < blocks - 2))
+        def _():
+            middle_gradient(size, h1t, ga2, t // 2 + 1, put)
+
+        @pl.when(jnp.logical_and(lax.rem(t, 2) == 1, t < 2 * tiles))
+        def _():
+            span = span_of(t // 2)
+            xt[:, span] = jnp.concatenate([x_ref[t - 1], x_ref[t]], axis=0).astype(jnp.bfloat16).T
+            ga1[span, :] = (mul_t(ga2[span, :], w2[...]) * s1[span, :].astype(jnp.float32)).astype(jnp.bfloat16)
+
+        @pl.when(t == blocks - 2)
+        def _():
+            last_gradient(size, h2t, gt, put)
+
+        @pl.when(t == blocks)
+        def _():
+            first_gradient(size, xt, ga1, put)
+
+        @pl.when(t == blocks + 2)
+        def _():
+            x2m.wait()
+
+            def put_final(lat, value):
+                final_ref[lat] = value
+
+            synthesise(size, (syn_hi[...], syn_lo[...]), got2m, put_final)
+
     x2m.drain()
     red.drain()
+    pltpu.make_async_copy(red.o, o_hbm, osem).wait()
+
+
+def unpack_kernel(hidden, features, o_hbm, g1_hbm, g2_hbm, g3_hbm, o, isem, osem):
+    blocks = hidden // LANES
+    rows = lambda b: pl.ds(b * CHUNK, CHUNK)
+    loads = [pltpu.make_async_copy(o_hbm.at[rows(b), :], o.at[rows(b), :], isem.at[b]) for b in range(blocks + 2)]
+    stores = [
+        pltpu.make_async_copy(o.at[rows(b), :], g2_hbm.at[:, pl.ds(b * LANES, LANES)], osem.at[0])
+        for b in range(blocks)
+    ] + [pltpu.make_async_copy(o.at[rows(blocks), :], g3_hbm, osem.at[1])]
+    firsts = [
+        pltpu.make_async_copy(o.at[pl.ds((blocks + 1) * CHUNK + b * features, features), :],
+                              g1_hbm.at[:, pl.ds(b * LANES, LANES)], osem.at[2])
+        for b in range(blocks)
+    ]
+    for load in loads:
+        load.start()
+    for load, store in zip(loads, stores):
+        load.wait()
+        store.start()
+    loads[-1].wait()
+    for store in firsts:
+        store.start()
+    for b, count in enumerate((blocks * CHUNK, CHUNK, CHUNK)):
+        pltpu.make_async_copy(o.at[pl.ds(0, count), :], o.at[pl.ds(0, count), :], osem.at[b]).wait()
 
 
 def fused_body(size, state, cotangent, w1, w2, w3):
@@ -747,16 +812,18 @@
                     buf(grads)]
         + [buf(blocks)] * 7 + [dma, dma] + Exchange.sems(size) * 4,
     )(q1, back_c, w1, w2, w3, table, quad, *ana_t, *syn_t, *ana)
-    reduce_scratch = Reduce.scratch(size.hidden // LANES + 2, size.bands // 4)
     final, totals = call(
-        last_kernel, 3, 4 * work, [vmem] * 7 + [hbm] * 5, [vmem, vmem], [field, grads],
-        [buf(tall), buf(wide), buf(tall), buf(wide), x_t, narrow, buf(wide), buf(wide), buf(blocks), dma((5,))]
-        + Exchange.sems(size) + reduce_scratch[:1] + reduce_scratch[2:],
+        last_kernel, 3, 4 * work, [vmem] * 7 + [hbm] * 5, [vmem, hbm], [field, grads],
+        [buf(tall), buf(wide), buf(tall), buf(wide), x_t, narrow, buf(wide), buf(wide), buf(blocks), dma((5,)), dma]
+        + Exchange.sems(size) + Reduce.scratch(size.hidden // LANES + 2, size.bands // 4),
     )(pulled0, x0, back_m, w2, w3, *syn, sums, *saved)
-    lanes = size.hidden // LANES
-    middle, last, first = totals[:lanes * CHUNK], totals[lanes * CHUNK:(lanes + 1) * CHUNK], totals[(lanes + 1) * CHUNK:]
-    unblock = lambda t, rows: t.reshape(lanes, rows, LANES).transpose(1, 0, 2).reshape(rows, size.hidden)
-    return final[None], unblock(first, size.features), unblock(middle, size.hidden), last
+    g1, g2, g3 = pl.pallas_call(
+        functools.partial(unpack_kernel, size.hidden, size.features),
+        in_specs=[hbm], out_specs=[hbm] * 3,
+        out_shape=[jax.ShapeDtypeStruct(w.shape, f32) for w in (w1, w2, w3)],
+        scratch_shapes=[buf(grads), dma((size.hidden // LANES + 2,)), dma((3,))],
+    )(totals)
+    return final[None], g1, g2, g3
 
 
 def np_halves(table):

time: 206 us -> 177 us (0.86)
  Pallas kernels: 197 us -> 175 us
  local copies, waits for them, and re-layouts: 8.94 us -> 0.98 us
    pallas_call x1 -> x2, Pallas kernels: 99.2 us -> 77.9 us  [the longest x1 73.2 us: fused_body(): call(last_kernel, 3, 4 * work, [vmem] * 7 + [hbm] * 5, [vmem, hbm], [fiel...]
    slice x2 -> x0, local copies, waits for them, and re-layouts: 4.52 us -> none  [the longest x1 2.46 us: fused_body(): totals[:lanes * CHUNK]]
    reshape x2 -> x0, local copies, waits for them, and re-layouts: 3.44 us -> none  [fused_body(): t.reshape(lanes, rows, LANES).transpose(1, 0, 2).reshape(rows, size.hidden)]
where the time goes in v3:
time: 177 us
  Pallas kernels  175 us (99%)
    pallas_call x1, Pallas kernels, fused_body(): call(last_kernel, 3, 4 * work, [vmem] * 7 + [hbm] * 5, [vmem, hbm], [fiel...  73.2 us
    pallas_call x1, Pallas kernels, fused_body(): call(middle_kernel, 2, 6 * work, [vmem] * 5 + [hbm] + [vmem] * 7, [vmem,...  56.6 us
    pallas_call x1, Pallas kernels, fused_body(): call(first_kernel, 1, 2 * work, [vmem] * 5 + [hbm] + [vmem] * 7, [vmem] *...  40.9 us
    pallas_call x1, Pallas kernels, fused_body(): pl.pallas_call(functools.partial(unpack_kernel, size.hidden, size.feature...  4.71 us

profile of v3, /device:TPU:1, one launch (start us, length us, event | category | flops | bytes accessed | tf_op | source)
XLA Modules:
  0.0 177.0 jit_solution(17330725021714477264)
XLA Ops:
  0.6 40.9 %shard_map.174 = (f32[8,256,128]{2,1,0:T(8,128)}, f32[1024,128]{1,0:T(8,128)}, bf16[1024,2048]{1,0:T(8,128)(2,1)}, bf16[2048,1024]{1,0:T(8,128)(2,1)}, bf16[1024...) custom-call(f32[8,256,128]{2,1,0:T(8,128)} %bitcast.5, f32[8,256,128]{2,1,0:T(8,128)} %bitcast.4, bf16[128,1024]{1,0:T(8,128)(2,1)} %w1.3, ...), custom_call_target="tpu_custom_call" | custom-call | flops 5368709120 | bytes 16777216 | tf_op jit(solution)/shard_map/pallas_call | solution.py:802
  41.5 56.6 %shard_map.175 = (f32[8,256,128]{2,1,0:T(8,128)}, f32[1024,128]{1,0:T(8,128)}, f32[10240,128]{1,0:T(8,128)}) custom-call(f32[8,256,128]{2,1,0:T(8,128)} %get-tuple-element.18.q_ref, f32[1024,128]{1,0:T(8,128)} %get-tuple-element.19.backc_ref, bf16[128,1024]{1,0:T(8,128)(2,1)} %w1.3, bf16[1024,1024]{1,0:T(8,128)(2,1)} %w2.5, bf16[1024,128]{1,0:T(8,128)(2,1)} %w3.5, ...), custom_call_target="tpu_custom_call" | custom-call | flops 16106127360 | bytes 16777216 | tf_op jit(solution)/shard_map/pallas_call | solution.py:808
  98.1 73.2 %shard_map.176 = (f32[8,256,128]{2,1,0:T(8,128)}, f32[10240,128]{1,0:T(8,128)}) custom-call(f32[8,256,128]{2,1,0:T(8,128)} %get-tuple-element.20.p_ref, f32[8,256,128]{2,1,0:T(8,128)} %bitcast.6, f32[1024,128]{1,0:T(8,128)} %get-tuple-element.21.backm_ref, bf16[1024,1024]{1,0:T(8,128)(2,1)} %w2.5, bf16[1024,128]{1,0:T(8,128)(2,1)} %w3.5, ...), custom_call_target="tpu_custom_call" | custom-call | flops 10737418240 | bytes 16777216 | tf_op jit(solution)/shard_map/pallas_call | solution.py:815
  171.3 0.0 copy-start
  171.3 4.7 %shard_map.177 = (f32[128,1024]{1,0:T(8,128)}, f32[1024,1024]{1,0:T(8,128)}, f32[1024,128]{1,0:T(8,128)}) custom-call(f32[10240,128]{1,0:T(8,128)} %get-tuple-element.28.o_hbm), custom_call_target="tpu_custom_call" | custom-call | tf_op jit(solution)/shard_map/pallas_call | solution.py:820
  176.0 0.0 copy-done
  176.1 1.0 copy.20
Async XLA Ops:
  171.3 4.7 %copy-start = (f32[8,256,128]{2,1,0:T(8,128)S(1)}, f32[8,256,128]{2,1,0:T(8,128)}, u32[]{:S(2)}) copy-start(f32[8,256,128]{2,1,0:T(8,128)} %get-tuple-element.27) | copy-start | bytes 3145732

commit v4 on v3

--- a/solution.py
+++ b/solution.py
@@ -164,6 +164,7 @@
 CHUNK = 1024
 SPAN = CHUNK
 HALF = SPAN // 2
+EARLY = 3
 LAGS = (0, 1, 3, 5, 7, 9, 11, 13, 14)
 
 
@@ -188,13 +189,12 @@
     pl.semaphore_signal(pltpu.get_barrier_semaphore(), inc=1, device_id=device, device_id_type=MESH_ID)
 
 
-def greet_reduce(place):
+def greet_all(place, bands):
     signal_to(place.across_core)
-    signal_to(place.across_x)
-    signal_to(place.across_y)
-    for step in range(1, place.depth):
-        signal_to(place.along_z(step)[1])
-    pl.semaphore_wait(pltpu.get_barrier_semaphore(), place.depth + 2)
+
+    @pl.loop(1, bands)
+    def _(step):
+        signal_to({"lat": lax.rem(place.me + step, bands)})
 
 
 def send(src, dst, ssem, rsem, device):
@@ -209,6 +209,7 @@
 
 class Reduce:
     SENDS = 8
+    REFS = 15
 
     @staticmethod
     def scratch(chunks, depth):
@@ -332,50 +333,12 @@
             wait_bytes(self.g.at[pl.ds(0, count * self.chunks), :], self.sent.at[i])
 
 
-def reduce_kernel(bands, g1_ref, g2_ref, g3_ref, o1_ref, o2_ref, o3_ref, *scratch):
-    place = Place(bands)
-    hidden = g2_ref.shape[1]
-    blocks = hidden // LANES
-    chunks = blocks + 2
-    red = Reduce(place, chunks, scratch)
-    greet_reduce(place)
-
-    for b in range(blocks):
-        red.g[pl.ds(b * CHUNK, CHUNK), :] = g2_ref[:, pl.ds(b * LANES, LANES)]
-        red.g[pl.ds((blocks + 1) * CHUNK + b * LANES, LANES), :] = g1_ref[:, pl.ds(b * LANES, LANES)]
-    red.g[pl.ds(blocks * CHUNK, CHUNK), :] = g3_ref[...]
-
-    @pl.loop(0, red.steps)
-    def _(t):
-        red.step(t)
-
-    for b in range(blocks):
-        o2_ref[:, pl.ds(b * LANES, LANES)] = red.o[pl.ds(b * CHUNK, CHUNK), :]
-        o1_ref[:, pl.ds(b * LANES, LANES)] = red.o[pl.ds((blocks + 1) * CHUNK + b * LANES, LANES), :]
-    o3_ref[...] = red.o[pl.ds(blocks * CHUNK, CHUNK), :]
-    red.drain()
-
-
 def fits_reduce(bands, pairs, features, hidden):
     return pairs == 2 and bands % 8 == 0 and bands <= 32 and features == LANES and hidden == CHUNK
 
 
 def reduce_totals(totals):
-    bands, pairs = lax.axis_size("lat"), lax.axis_size("dp")
-    features, hidden = totals[0].shape
-    if not fits_reduce(bands, pairs, features, hidden):
-        return lax.psum(tuple(totals), ("lat", "dp"))
-    vmem = pl.BlockSpec(memory_space=pltpu.VMEM)
-    return pl.pallas_call(
-        functools.partial(reduce_kernel, bands),
-        in_specs=[vmem] * 3,
-        out_specs=[vmem] * 3,
-        out_shape=[jax.ShapeDtypeStruct(t.shape, t.dtype) for t in totals],
-        scratch_shapes=Reduce.scratch(hidden // LANES + 2, bands // 4),
-        compiler_params=pltpu.CompilerParams(
-            collective_id=3, has_side_effects=True, vmem_limit_bytes=56 * 2**20
-        ),
-    )(*totals)
+    return lax.psum(tuple(totals), ("lat", "dp"))
 
 
 def split_dot(high_low, value, turned=False):
@@ -396,21 +359,26 @@
         self.bands, self.lat_rows, self.lon = bands, lat_rows, lon
         self.features, self.hidden = features, hidden
         self.lats = bands * lat_rows
-        self.waves = MW // bands
-        self.pairs = 2 * self.waves
+        self.team = bands // 2
+        self.half_lats = self.lats // 2
+        self.couples = MW // 2 // self.team
+        self.pairs = 4 * self.couples
         self.block = self.pairs * lat_rows
         self.rows = lat_rows * lon
         self.all_pairs = 2 * MW
+        self.degrees = (MW + 1 + 7) // 8 * 8
 
 
 class Exchange:
     @staticmethod
     def sems(size):
-        return [pltpu.SemaphoreType.DMA, pltpu.SemaphoreType.DMA((size.bands,))]
+        return [pltpu.SemaphoreType.DMA, pltpu.SemaphoreType.DMA((size.team,))]
 
     def __init__(self, size, out, got, ssem, rsem):
         self.size, self.out, self.got, self.ssem, self.rsem = size, out, got, ssem, rsem
-        self.me = lax.axis_index("lat")
+        me = lax.axis_index("lat")
+        self.me = lax.rem(me, size.team)
+        self.base = me - self.me
 
     def part(self, ref, band, first, count):
         return ref.at[pl.ds(pl.multiple_of(band * self.size.block + first, 8), count), :]
@@ -418,60 +386,103 @@
     def start(self, first=0, count=None):
         count = self.size.block if count is None else count
 
-        @pl.loop(1, self.size.bands)
+        @pl.loop(1, self.size.team)
         def _(step):
-            to = lax.rem(self.me + step, self.size.bands)
+            to = lax.rem(self.me + step, self.size.team)
             send(self.part(self.out, to, first, count), self.part(self.got, self.me, first, count),
-                 self.ssem, self.rsem.at[step], {"lat": to})
+                 self.ssem, self.rsem.at[step], {"lat": self.base + to})
 
         self.part(self.got, self.me, first, count)[...] = self.part(self.out, self.me, first, count)[...]
 
     def wait(self):
-        @pl.loop(1, self.size.bands)
+        @pl.loop(1, self.size.team)
         def _(step):
             wait_bytes(self.part(self.got, 0, 0, self.size.block), self.rsem.at[step])
 
     def drain(self):
-        wait_bytes(self.out.at[pl.ds(0, (self.size.bands - 1) * self.size.block), :], self.ssem)
-
-
-def greet_lat(size, also=0):
-    me = lax.axis_index("lat")
-
-    @pl.loop(1, size.bands)
-    def _(step):
-        signal_to({"lat": lax.rem(me + step, size.bands)})
+        wait_bytes(self.out.at[pl.ds(0, (self.size.team - 1) * self.size.block), :], self.ssem)
+
+
+class Swap:
+    @staticmethod
+    def sems(size):
+        return [pltpu.SemaphoreType.DMA((size.couples,)), pltpu.SemaphoreType.DMA((size.couples,))]
+
+    def __init__(self, size, out, got, ssem, rsem):
+        self.size, self.out, self.got, self.ssem, self.rsem = size, out, got, ssem, rsem
+
+    def part(self, ref, couple):
+        return ref.at[pl.ds(couple * 2 * self.size.degrees, 2 * self.size.degrees), :]
+
+    def start(self, couple):
+        send(self.part(self.out, couple), self.part(self.got, couple),
+             self.ssem.at[couple], self.rsem.at[couple], {"lat": opposite(self.size)})
+
+    def wait(self, couple):
+        wait_bytes(self.part(self.got, couple), self.rsem.at[couple])
+
+    def drain(self, couple):
+        wait_bytes(self.part(self.out, couple), self.ssem.at[couple])
+
+
+def opposite(size):
+    return lax.rem(lax.axis_index("lat") + size.team, size.bands)
 
 
 def greeted(count):
     pl.semaphore_wait(pltpu.get_barrier_semaphore(), count)
 
 
-def build_operator(size, table_ref, quad_ref, op_hi, op_lo):
-    quad = quad_ref[...]
-    for m in range(size.waves):
-        table = table_ref[m]
-        base = split_dot(halves(table), table, turned=True)
-        hi, lo = halves(base * quad)
-        op_hi[m] = hi
-        op_lo[m] = lo
-
-
-def legendre(size, op_hi, op_lo, got, out, turned):
-    for m in range(size.waves):
-        value = jnp.concatenate(
-            [got[pl.ds(2 * m + p, size.lats, stride=size.pairs), :] for p in (0, 1)], axis=1)
-        back = split_dot((op_hi[m], op_lo[m]), value, turned)
+def build_tables(size, table_ref, quad_ref, plain_hi, plain_lo, quad_hi, quad_lo):
+    north = lax.axis_index("lat") // size.team
+    width, lats = 2 * size.half_lats, size.half_lats
+    source = lax.broadcasted_iota(jnp.int32, (width, width), 0)
+    column = lax.broadcasted_iota(jnp.int32, (width, width), 1)
+    first = jnp.where(column >= lats, lats, 0)
+    mirrored = 2 * first + (lats - 1) - column
+    turn = jnp.where(source == jnp.where(north == 1, mirrored, column), 1.0, 0.0).astype(jnp.bfloat16)
+    degree = lax.broadcasted_iota(jnp.int32, (size.degrees, width), 0)
+    sign = jnp.where(jnp.logical_and(north == 1, lax.rem(degree, 2) == 1), -1.0, 1.0)
+    for i in range(size.couples):
+        table = table_ref[i] * sign
+        for value, hi_ref, lo_ref in ((table, plain_hi, plain_lo), (table * quad_ref[...], quad_hi, quad_lo)):
+            for part, ref in zip(halves(value), (hi_ref, lo_ref)):
+                ref[i] = plain_dot(part, turn).astype(jnp.bfloat16)
+
+
+def half_sums(size, table, got, swap, couples):
+    for i in range(size.couples):
+        value = jnp.concatenate([
+            jnp.concatenate(
+                [got[pl.ds(4 * i + 2 * w + p, size.half_lats, stride=size.pairs), :] for p in (0, 1)], axis=1)
+            for w in (0, 1)], axis=0)
+        coef = split_dot((table[0][i], table[1][i]), value)
         for p in (0, 1):
-            for d in range(size.bands):
-                out[pl.ds(d * size.block + (2 * m + p) * size.lat_rows, size.lat_rows), :] = (
-                    back[d * size.lat_rows:(d + 1) * size.lat_rows, p * LANES:(p + 1) * LANES])
+            swap.out[pl.ds((2 * i + p) * size.degrees, size.degrees), :] = coef[:, p * LANES:(p + 1) * LANES]
+        if i < couples:
+            swap.start(i)
+
+
+def from_coefs(size, table, swap, exchange):
+    for i in range(size.couples):
+        swap.wait(i)
+        value = jnp.concatenate([
+            swap.out[pl.ds((2 * i + p) * size.degrees, size.degrees), :]
+            + swap.got[pl.ds((2 * i + p) * size.degrees, size.degrees), :] for p in (0, 1)], axis=1)
+        back = split_dot((table[0][i], table[1][i]), value, True)
+        for w in (0, 1):
+            for p in (0, 1):
+                for d in range(size.team):
+                    row = w * size.half_lats + d * size.lat_rows
+                    exchange.out[pl.ds(d * size.block + (4 * i + 2 * w + p) * size.lat_rows, size.lat_rows), :] = (
+                        back[row:row + size.lat_rows, p * LANES:(p + 1) * LANES])
+        exchange.start(4 * i * size.lat_rows, 4 * size.lat_rows)
 
 
 def analyse(size, high_low, first, second, lat, out):
     wav = split_dot(high_low, jnp.concatenate([first, second], axis=1))
     for u in (0, 1):
-        for d in range(size.bands):
+        for d in range(size.team):
             out[pl.ds(pl.multiple_of(d * size.block + (lat + u) * size.pairs, 8), size.pairs), :] = (
                 wav[d * size.pairs:(d + 1) * size.pairs, u * LANES:(u + 1) * LANES])
 
@@ -503,63 +514,7 @@
 
 
 def table_copy(size, table_hbm, table_ref, sem):
-    waves = size.waves
-    return pltpu.make_async_copy(table_hbm.at[pl.ds(lax.axis_index("lat") * waves, waves)], table_ref, sem)
-
-
-def first_kernel(size, x_ref, c_ref, w1, w2, w3, table_hbm, quad, ana_hi, ana_lo, syt_hi, syt_lo, syn_hi, syn_lo,
-                 q_ref, backc_ref, h1t_hbm, s1_hbm, h2t_hbm, s2_hbm,
-                 table, op_hi, op_lo, h1t, s1, h2t, s2, outc, gotc, outm, gotm, backm, got2m,
-                 tsem, ksems, *sems):
-    xc = Exchange(size, outc, gotc, *sems[0:2])
-    xm = Exchange(size, outm, gotm, *sems[2:4])
-    x2 = Exchange(size, backm, got2m, *sems[4:6])
-    greet_lat(size)
-    table_in = table_copy(size, table_hbm, table, tsem)
-    table_in.start()
-
-    @pl.loop(0, size.lat_rows // 2)
-    def _(i):
-        analyse(size, (syt_hi[...], syt_lo[...]), c_ref[2 * i], c_ref[2 * i + 1], 2 * i, outc)
-
-    greeted(size.bands - 1)
-    xc.start()
-    table_in.wait()
-    build_operator(size, table, quad, op_hi, op_lo)
-    keeps = ((h1t, h1t_hbm, 1), (s1, s1_hbm, 0), (h2t, h2t_hbm, 1), (s2, s2_hbm, 0))
-
-    def keep_copies(i):
-        span = pl.ds(pl.multiple_of(i * 2 * size.lon, 2 * size.lon), 2 * size.lon)
-        for k, (src, dst, axis) in enumerate(keeps):
-            where = (slice(None), span) if axis else (span, slice(None))
-            pltpu.make_async_copy(src.at[where], dst.at[where], ksems.at[k]).start()
-
-    @pl.loop(0, size.lat_rows // 2)
-    def _(i):
-        moved = [
-            forward_tile(size, pl.multiple_of((2 * i + u) * size.lon, size.lon), x_ref[2 * i + u],
-                         w1, w2, w3, (h1t, s1, h2t, s2, None))
-            for u in (0, 1)
-        ]
-        analyse(size, (ana_hi[...], ana_lo[...]), moved[0], moved[1], 2 * i, outm)
-        xm.start(pl.multiple_of(2 * i * size.pairs, 2 * size.pairs), 2 * size.pairs)
-        keep_copies(i)
-
-    xc.wait()
-    legendre(size, op_hi, op_lo, gotc, backc_ref, True)
-    xm.wait()
-    legendre(size, op_hi, op_lo, gotm, backm, False)
-    x2.start()
-    x2.wait()
-
-    def put(lat, value):
-        q_ref[lat] = value
-
-    synthesise(size, (syn_hi[...], syn_lo[...]), got2m, put)
-    for x in (xc, xm, x2):
-        x.drain()
-    for k, (src, dst, _) in enumerate(keeps):
-        pltpu.make_async_copy(src, dst, ksems.at[k]).wait()
+    return pltpu.make_async_copy(table_hbm.at[lax.rem(lax.axis_index("lat"), size.team)], table_ref, sem)
 
 
 def plain_dot(a, b):
@@ -569,7 +524,7 @@
 def last_gradient(size, h2t, gt, put):
     half = size.hidden // 2
     for top in (0, half):
-        put(size.hidden // LANES * CHUNK + top, plain_dot(h2t[pl.ds(top, half), :], gt[...]))
+        put(top, plain_dot(h2t[pl.ds(top, half), :], gt[...]))
 
 
 def middle_gradient(size, h1t, ga2, i, put):
@@ -578,7 +533,7 @@
     for top in (0, half):
         part = plain_dot(h1t[pl.ds(top, half), :], ga2[:, columns])
         for u in (0, 1):
-            put(pl.multiple_of((2 * i + u) * CHUNK + top, half), part[:, u * LANES:(u + 1) * LANES])
+            put(pl.multiple_of((2 * i + u + 1) * CHUNK + top, half), part[:, u * LANES:(u + 1) * LANES])
 
 
 def first_gradient(size, xt, ga1, put):
@@ -599,44 +554,107 @@
     first_gradient(size, xt, ga1, put)
 
 
-def middle_kernel(size, q_ref, backc_ref, w1, w2, w3, table_hbm, quad,
-                  ana_hi, ana_lo, syt_hi, syt_lo, ant_hi, ant_lo,
-                  p_ref, backm_ref, g_hbm,
-                  table, op_hi, op_lo, h1t, s1, h2t, s2, xt, pulled, gt, ga1, ga2, g,
-                  got2c, outm, gotm, outg, gotg, backg, got2g, tsem, gsem, *sems):
-    x2c = Exchange(size, backc_ref, got2c, *sems[0:2])
-    xm = Exchange(size, outm, gotm, *sems[2:4])
-    xg = Exchange(size, outg, gotg, *sems[4:6])
-    x2g = Exchange(size, backg, got2g, *sems[6:8])
-    greet_lat(size)
-    table_in = table_copy(size, table_hbm, table, tsem)
-    table_in.start()
-    greeted(size.bands - 1)
-    x2c.start()
-    table_in.wait()
-    build_operator(size, table, quad, op_hi, op_lo)
-
-    @pl.loop(0, size.lat_rows // 2)
+def whole_kernel(size, x_hbm, c_hbm, w1_hbm, w2_hbm, w3_hbm, table_hbm, quad,
+                 ana_hi, ana_lo, syt_hi, syt_lo, syn_hi, syn_lo, ant_hi, ant_lo,
+                 final_hbm, o_hbm, h1t_hbm, s1_hbm, h2t_hbm, s2_hbm, *scratch):
+    (x, c, w1, w2, w3, table, p_hi, p_lo, u_hi, u_lo, h1t, s1, h2t, s2, xt0, xt1, gt, ga1, ga2,
+     isems, ksems, lsems, fsem, osem) = scratch[:24]
+    scratch = list(scratch[24:])
+
+    def take(count):
+        taken = scratch[:count]
+        del scratch[:count]
+        return taken
+
+    place = Place(size.bands)
+    blocks = size.hidden // LANES
+    tiles = size.lat_rows // 2
+    red = Reduce(place, blocks + 2, take(Reduce.REFS))
+    g = red.g
+    to_c, to_m0, to_m1, to_g = [Exchange(size, *take(4)) for _ in range(4)]
+    fro_c, fro_m0, fro_m1, fro_g = [Exchange(size, *take(4)) for _ in range(4)]
+    swap_c, swap_m0, swap_m1, swap_g = [Swap(size, *take(4)) for _ in range(4)]
+    plain, quads = (p_hi, p_lo), (u_hi, u_lo)
+
+    greet_all(place, size.bands)
+    inputs = [pltpu.make_async_copy(src, dst, isems.at[k]) for k, (src, dst) in enumerate(
+        ((c_hbm, c), (x_hbm, x), (w1_hbm, w1), (w2_hbm, w2), (w3_hbm, w3)))]
+    inputs.append(table_copy(size, table_hbm, table, isems.at[5]))
+    for copy in inputs:
+        copy.start()
+
+    def span_of(i):
+        return pl.ds(pl.multiple_of(2 * i * size.lon, 2 * size.lon), 2 * size.lon)
+
+    def start_tile(exchange, i):
+        exchange.start(pl.multiple_of(2 * i * size.pairs, 2 * size.pairs), 2 * size.pairs)
+
+    def store_in(ref):
+        def put(lat, value):
+            ref[lat] = value
+        return put
+
+    inputs[0].wait()
+
+    @pl.loop(0, tiles)
     def _(i):
+        analyse(size, (syt_hi[...], syt_lo[...]), c[2 * i], c[2 * i + 1], 2 * i, to_c.out)
+
+    greeted(size.bands)
+    to_c.start()
+    for copy in inputs[1:]:
+        copy.wait()
+    build_tables(size, table, quad, *plain, *quads)
+    keeps = ((h1t, h1t_hbm, 1), (s1, s1_hbm, 0), (h2t, h2t_hbm, 1), (s2, s2_hbm, 0))
+
+    def forward(i, xt, exchange):
         moved = [
-            forward_tile(size, pl.multiple_of((2 * i + u) * size.lon, size.lon), q_ref[2 * i + u],
+            forward_tile(size, pl.multiple_of((2 * i + u) * size.lon, size.lon), x[2 * i + u],
                          w1, w2, w3, (h1t, s1, h2t, s2, xt))
             for u in (0, 1)
         ]
-        analyse(size, (ana_hi[...], ana_lo[...]), moved[0], moved[1], 2 * i, outm)
-
-    x2c.wait()
-
-    def put(lat, value):
-        pulled[lat] = value
-
-    synthesise(size, (ant_hi[...], ant_lo[...]), got2c, put)
-    xm.start()
-
-    @pl.loop(0, size.lat_rows // 2)
+        analyse(size, (ana_hi[...], ana_lo[...]), moved[0], moved[1], 2 * i, exchange.out)
+        start_tile(exchange, i)
+
+    @pl.loop(0, tiles)
     def _(i):
-        span = pl.ds(pl.multiple_of(2 * i * size.lon, 2 * size.lon), 2 * size.lon)
-        p = jnp.concatenate([pulled[2 * i], pulled[2 * i + 1]], axis=0)
+        @pl.when(i == tiles - 1)
+        def _():
+            to_c.wait()
+            half_sums(size, plain, to_c.got, swap_c, EARLY)
+
+        forward(i, xt0, to_m0)
+        for k, (src, dst, axis) in enumerate(keeps):
+            where = (slice(None), span_of(i)) if axis else (span_of(i), slice(None))
+            pltpu.make_async_copy(src.at[where], dst.at[where], ksems.at[k]).start()
+
+    to_m0.wait()
+    half_sums(size, quads, to_m0.got, swap_m0, size.couples)
+    for i in range(EARLY, size.couples):
+        swap_c.start(i)
+    from_coefs(size, plain, swap_m0, fro_m0)
+    from_coefs(size, quads, swap_c, fro_c)
+    for k, (src, dst, _) in enumerate(keeps):
+        pltpu.make_async_copy(src, dst, ksems.at[k]).wait()
+    fro_m0.wait()
+    synthesise(size, (syn_hi[...], syn_lo[...]), fro_m0.got, store_in(x))
+
+    @pl.loop(0, tiles)
+    def _(i):
+        forward(i, xt1, to_m1)
+
+    fro_c.wait()
+    synthesise(size, (ant_hi[...], ant_lo[...]), fro_c.got, store_in(c))
+
+    @pl.loop(0, tiles)
+    def _(i):
+        @pl.when(i == 1)
+        def _():
+            to_m1.wait()
+            half_sums(size, quads, to_m1.got, swap_m1, size.couples)
+
+        span = span_of(i)
+        p = jnp.concatenate([c[2 * i], c[2 * i + 1]], axis=0)
         g_t = (tend_weight * p).astype(jnp.bfloat16)
         gt[span, :] = g_t
         g_a2 = (mul_t(g_t, w3[...]) * s2[span, :].astype(jnp.float32)).astype(jnp.bfloat16)
@@ -644,66 +662,40 @@
         g_a1 = (mul_t(g_a2, w2[...]) * s1[span, :].astype(jnp.float32)).astype(jnp.bfloat16)
         ga1[span, :] = g_a1
         grad = p + mul_t(g_a1, w1[...])
-        analyse(size, (syt_hi[...], syt_lo[...]), grad[:size.lon], grad[size.lon:], 2 * i, outg)
-        xg.start(pl.multiple_of(2 * i * size.pairs, 2 * size.pairs), 2 * size.pairs)
+        analyse(size, (syt_hi[...], syt_lo[...]), grad[:size.lon], grad[size.lon:], 2 * i, to_g.out)
+        start_tile(to_g, i)
+
+    loads = [pltpu.make_async_copy(src, dst, lsems.at[k]) for k, (dst, src, _) in enumerate(keeps)]
+    loads[3].start()
+    loads[1].start()
 
     def keep(row, value):
         g[pl.ds(row, value.shape[0]), :] = value
 
-    weight_gradients(size, h1t, h2t, xt, gt, ga1, ga2, keep)
-    xm.wait()
-    legendre(size, op_hi, op_lo, gotm, backm_ref, False)
-    g_out = pltpu.make_async_copy(g, g_hbm, gsem)
-    g_out.start()
-    xg.wait()
-    legendre(size, op_hi, op_lo, gotg, backg, True)
-    x2g.start()
-    x2g.wait()
-
-    def put_pulled(lat, value):
-        p_ref[lat] = value
-
-    synthesise(size, (ant_hi[...], ant_lo[...]), got2g, put_pulled)
-    for x in (x2c, xm, xg, x2g):
-        x.drain()
-    g_out.wait()
-
-
-def last_kernel(size, p_ref, x_ref, backm_ref, w2, w3, syn_hi, syn_lo, g_hbm, h1t_hbm, s1_hbm, h2t_hbm, s2_hbm,
-                final_ref, o_hbm, h1t, s1, h2t, s2, xt, gt, ga1, ga2, got2m, lsems, osem, ssem, rsem, *scratch):
-    place = Place(size.bands)
-    blocks = size.hidden // LANES
-    tiles = size.lat_rows // 2
-    red = Reduce(place, blocks + 2, scratch)
-    g = red.g
-    x2m = Exchange(size, backm_ref, got2m, ssem, rsem)
-    greet_lat(size)
-    signal_to(place.across_core)
-    loads = [pltpu.make_async_copy(src, dst, lsems.at[k]) for k, (src, dst) in enumerate(
-        ((s2_hbm, s2), (g_hbm, g), (h1t_hbm, h1t), (h2t_hbm, h2t), (s1_hbm, s1)))]
-    for load in loads:
-        load.start()
-    greeted(size.bands)
-    x2m.start()
-    loads[0].wait()
-
-    def span_of(i):
-        return pl.ds(pl.multiple_of(2 * i * size.lon, 2 * size.lon), 2 * size.lon)
+    to_g.wait()
+    half_sums(size, plain, to_g.got, swap_g, size.couples)
+    from_coefs(size, plain, swap_m1, fro_m1)
+    weight_gradients(size, h1t, h2t, xt1, gt, ga1, ga2, keep)
+    loads[2].start()
+    loads[0].start()
+    fro_m1.wait()
+    synthesise(size, (syn_hi[...], syn_lo[...]), fro_m1.got, store_in(x))
+    final_copy = pltpu.make_async_copy(x, final_hbm, fsem)
+    final_copy.start()
+    from_coefs(size, quads, swap_g, fro_g)
+    fro_g.wait()
+    synthesise(size, (ant_hi[...], ant_lo[...]), fro_g.got, store_in(c))
 
     @pl.loop(0, tiles)
     def _(i):
-        span = span_of(i)
-        g_t = (tend_weight * jnp.concatenate([p_ref[2 * i], p_ref[2 * i + 1]], axis=0)).astype(jnp.bfloat16)
-        gt[span, :] = g_t
-        ga2[span, :] = (mul_t(g_t, w3[...]) * s2[span, :].astype(jnp.float32)).astype(jnp.bfloat16)
-
-    for load in loads[1:]:
-        load.wait()
+        gt[span_of(i), :] = (tend_weight * jnp.concatenate([c[2 * i], c[2 * i + 1]], axis=0)).astype(jnp.bfloat16)
 
     def put(row, value):
         g[pl.ds(row, value.shape[0]), :] += value
 
-    middle_gradient(size, h1t, ga2, 0, put)
+    for load in loads:
+        load.wait()
+    last_gradient(size, h2t, gt, put)
 
     @pl.loop(0, red.steps)
     def _(t):
@@ -714,116 +706,127 @@
             rows = pl.ds(pl.multiple_of((t - LAGS[-1]) * CHUNK, CHUNK), CHUNK)
             pltpu.make_async_copy(red.o.at[rows, :], o_hbm.at[rows, :], osem).start()
 
-        @pl.when(jnp.logical_and(lax.rem(t, 2) == 0, t < blocks - 2))
+        @pl.when(t == 0)
         def _():
-            middle_gradient(size, h1t, ga2, t // 2 + 1, put)
+            @pl.loop(0, tiles)
+            def _(i):
+                span = span_of(i)
+                ga2[span, :] = (mul_t(gt[span, :], w3[...]) * s2[span, :].astype(jnp.float32)).astype(jnp.bfloat16)
+
+        @pl.when(jnp.logical_and(lax.rem(t, 2) == 0, t < blocks))
+        def _():
+            middle_gradient(size, h1t, ga2, t // 2, put)
 
         @pl.when(jnp.logical_and(lax.rem(t, 2) == 1, t < 2 * tiles))
         def _():
             span = span_of(t // 2)
-            xt[:, span] = jnp.concatenate([x_ref[t - 1], x_ref[t]], axis=0).astype(jnp.bfloat16).T
             ga1[span, :] = (mul_t(ga2[span, :], w2[...]) * s1[span, :].astype(jnp.float32)).astype(jnp.bfloat16)
-
-        @pl.when(t == blocks - 2)
-        def _():
-            last_gradient(size, h2t, gt, put)
 
         @pl.when(t == blocks)
         def _():
-            first_gradient(size, xt, ga1, put)
-
-        @pl.when(t == blocks + 2)
-        def _():
-            x2m.wait()
-
-            def put_final(lat, value):
-                final_ref[lat] = value
-
-            synthesise(size, (syn_hi[...], syn_lo[...]), got2m, put_final)
-
-    x2m.drain()
+            first_gradient(size, xt0, ga1, put)
+
+    for exchange in (to_c, to_m0, to_m1, to_g, fro_c, fro_m0, fro_m1, fro_g):
+        exchange.drain()
+    for swap in (swap_c, swap_m0, swap_m1, swap_g):
+        for i in range(size.couples):
+            swap.drain(i)
     red.drain()
+    final_copy.wait()
     pltpu.make_async_copy(red.o, o_hbm, osem).wait()
 
 
-def unpack_kernel(hidden, features, o_hbm, g1_hbm, g2_hbm, g3_hbm, o, isem, osem):
+def unpack_kernel(hidden, features, f_hbm, o_hbm, final_hbm, g1_hbm, g2_hbm, g3_hbm, f, o, isem, osem):
     blocks = hidden // LANES
     rows = lambda b: pl.ds(b * CHUNK, CHUNK)
+    load_f = pltpu.make_async_copy(f_hbm, f, isem.at[blocks + 2])
     loads = [pltpu.make_async_copy(o_hbm.at[rows(b), :], o.at[rows(b), :], isem.at[b]) for b in range(blocks + 2)]
-    stores = [
-        pltpu.make_async_copy(o.at[rows(b), :], g2_hbm.at[:, pl.ds(b * LANES, LANES)], osem.at[0])
+    stores = [pltpu.make_async_copy(o.at[rows(0), :], g3_hbm, osem.at[1])] + [
+        pltpu.make_async_copy(o.at[rows(b + 1), :], g2_hbm.at[:, pl.ds(b * LANES, LANES)], osem.at[0])
         for b in range(blocks)
-    ] + [pltpu.make_async_copy(o.at[rows(blocks), :], g3_hbm, osem.at[1])]
+    ]
     firsts = [
         pltpu.make_async_copy(o.at[pl.ds((blocks + 1) * CHUNK + b * features, features), :],
                               g1_hbm.at[:, pl.ds(b * LANES, LANES)], osem.at[2])
         for b in range(blocks)
     ]
+    store_f = pltpu.make_async_copy(f, final_hbm, osem.at[3])
     for load in loads:
         load.start()
+    load_f.start()
     for load, store in zip(loads, stores):
         load.wait()
         store.start()
     loads[-1].wait()
     for store in firsts:
         store.start()
+    load_f.wait()
+    store_f.start()
     for b, count in enumerate((blocks * CHUNK, CHUNK, CHUNK)):
         pltpu.make_async_copy(o.at[pl.ds(0, count), :], o.at[pl.ds(0, count), :], osem.at[b]).wait()
+    store_f.wait()
+
+
+def packed_tables(size):
+    table, quad = legendre_tables(size.lats, MW)
+    lats = size.half_lats
+    packed = np.zeros((size.team, size.couples, size.degrees, 2 * lats), np.float32)
+    order = []
+    for d in range(size.team):
+        for i in range(size.couples):
+            m = d + size.team * i
+            other = MW - 1 - m
+            packed[d, i, :MW - m, :lats] = table[m, :MW - m, :lats]
+            packed[d, i, MW - m:MW + 1, lats:] = table[other, m::-1, :lats]
+            order += [2 * m, 2 * m + 1, 2 * other, 2 * other + 1]
+    return packed, np.concatenate([quad[:lats]] * 2)[None, :], np.asarray(order)
 
 
 def fused_body(size, state, cotangent, w1, w2, w3):
     analysis, synthesis = grid_tables(size.lon, MW)
-    table, quad = legendre_tables(size.lats, MW)
+    table, quad, order = packed_tables(size)
+    analysis, synthesis = analysis[:, order], synthesis[:, order]
     pair = lambda t: [jnp.asarray(part) for part in np_halves(t)]
     ana_t, syn_t = pair(analysis.T), pair(synthesis.T)
     ana, syn = pair(analysis), pair(synthesis)
-    table, quad = jnp.asarray(table), jnp.asarray(quad)[None, :]
+    table, quad = jnp.asarray(table), jnp.asarray(quad)
     vmem = pl.BlockSpec(memory_space=pltpu.VMEM)
     hbm = pl.BlockSpec(memory_space=pl.ANY)
     f32, bf16 = jnp.float32, jnp.bfloat16
     field = jax.ShapeDtypeStruct(state.shape[1:], f32)
-    blocks = jax.ShapeDtypeStruct((size.bands * size.block, LANES), f32)
+    blocks = jax.ShapeDtypeStruct((size.team * size.block, LANES), f32)
+    coefs = jax.ShapeDtypeStruct((2 * size.couples * size.degrees, LANES), f32)
     wide = jax.ShapeDtypeStruct((size.rows, size.hidden), bf16)
     tall = jax.ShapeDtypeStruct((size.hidden, size.rows), bf16)
     grads = jax.ShapeDtypeStruct(((size.hidden // LANES + 2) * CHUNK, LANES), f32)
     buf = lambda shape: pltpu.VMEM(shape.shape, shape.dtype)
     dma = pltpu.SemaphoreType.DMA
-    operator = [pltpu.VMEM((size.waves, MW, size.lats), f32)] + [
-        pltpu.VMEM((size.waves, size.lats, size.lats), bf16)] * 2
+    packed = (size.couples, size.degrees, 2 * size.half_lats)
+    tables = [pltpu.VMEM(packed, f32)] + [pltpu.VMEM(packed, bf16)] * 4
     narrow = pltpu.VMEM((size.rows, LANES), bf16)
     x_t = pltpu.VMEM((LANES, size.rows), bf16)
     work = size.rows * size.hidden * (size.hidden + 2 * size.features)
-    call = lambda kernel, ident, flops, ins, outs, shapes, scratch: pl.pallas_call(
-        functools.partial(kernel, size), in_specs=ins, out_specs=outs, out_shape=shapes, scratch_shapes=scratch,
-        cost_estimate=pl.CostEstimate(flops=flops, bytes_accessed=2**24, transcendentals=0),
+    final, totals, *_ = pl.pallas_call(
+        functools.partial(whole_kernel, size),
+        in_specs=[hbm] * 6 + [vmem] * 9,
+        out_specs=[hbm] * 6,
+        out_shape=[field, grads, tall, wide, tall, wide],
+        scratch_shapes=[buf(field), buf(field), buf(w1), buf(w2), buf(w3)] + tables
+        + [buf(tall), buf(wide), buf(tall), buf(wide), x_t, x_t, narrow, buf(wide), buf(wide)]
+        + [dma((6,)), dma((4,)), dma((4,)), dma, dma]
+        + Reduce.scratch(size.hidden // LANES + 2, size.bands // 4)
+        + ([buf(blocks)] * 2 + Exchange.sems(size)) * 8 + ([buf(coefs)] * 2 + Swap.sems(size)) * 4,
+        cost_estimate=pl.CostEstimate(flops=12 * work, bytes_accessed=2**25, transcendentals=0),
         compiler_params=pltpu.CompilerParams(
-            collective_id=ident, has_side_effects=True, vmem_limit_bytes=60 * 2**20))
-    x0 = state[0]
-    q1, back_c, *saved = call(
-        first_kernel, 1, 2 * work, [vmem] * 5 + [hbm] + [vmem] * 7, [vmem] * 2 + [hbm] * 4,
-        [field, blocks, tall, wide, tall, wide],
-        operator + [buf(tall), buf(wide), buf(tall), buf(wide)] + [buf(blocks)] * 6
-        + [dma, dma((4,))] + Exchange.sems(size) * 3,
-    )(x0, cotangent[0], w1, w2, w3, table, quad, *ana_t, *syn_t, *syn)
-    pulled0, back_m, sums = call(
-        middle_kernel, 2, 6 * work, [vmem] * 5 + [hbm] + [vmem] * 7, [vmem, vmem, hbm],
-        [field, blocks, grads],
-        operator + [buf(tall), buf(wide), buf(tall), buf(wide), x_t, buf(field), narrow, buf(wide), buf(wide),
-                    buf(grads)]
-        + [buf(blocks)] * 7 + [dma, dma] + Exchange.sems(size) * 4,
-    )(q1, back_c, w1, w2, w3, table, quad, *ana_t, *syn_t, *ana)
-    final, totals = call(
-        last_kernel, 3, 4 * work, [vmem] * 7 + [hbm] * 5, [vmem, hbm], [field, grads],
-        [buf(tall), buf(wide), buf(tall), buf(wide), x_t, narrow, buf(wide), buf(wide), buf(blocks), dma((5,)), dma]
-        + Exchange.sems(size) + Reduce.scratch(size.hidden // LANES + 2, size.bands // 4),
-    )(pulled0, x0, back_m, w2, w3, *syn, sums, *saved)
-    g1, g2, g3 = pl.pallas_call(
+            collective_id=1, has_side_effects=True, vmem_limit_bytes=63 * 2**20),
+    )(state[0], cotangent[0], w1, w2, w3, table, quad, *ana_t, *syn_t, *syn, *ana)
+    final, *grads_out = pl.pallas_call(
         functools.partial(unpack_kernel, size.hidden, size.features),
-        in_specs=[hbm], out_specs=[hbm] * 3,
-        out_shape=[jax.ShapeDtypeStruct(w.shape, f32) for w in (w1, w2, w3)],
-        scratch_shapes=[buf(grads), dma((size.hidden // LANES + 2,)), dma((3,))],
-    )(totals)
-    return final[None], g1, g2, g3
+        in_specs=[hbm] * 2, out_specs=[hbm] * 4,
+        out_shape=[field] + [jax.ShapeDtypeStruct(w.shape, f32) for w in (w1, w2, w3)],
+        scratch_shapes=[buf(field), buf(grads), dma((size.hidden // LANES + 3,)), dma((4,))],
+    )(final, totals)
+    return (final[None], *grads_out)
 
 
 def np_halves(table):
@@ -832,8 +835,8 @@
 
 
 def fits_fused(size, sample):
-    return (sample == 1 and size.lat_rows == 8 and size.pairs == 8 and size.lon % 256 == 0
-            and size.lats % LANES == 0 and size.bands % 8 == 0)
+    return (sample == 1 and size.lat_rows == 8 and size.pairs % 8 == 0 and size.lon % 256 == 0
+            and size.lats == LANES and size.bands % 8 == 0)
 
 
 def body(state, cotangent, w1, w2, w3):

time: 177 us -> 159 us (0.90)
  Pallas kernels: 175 us -> 158 us
    pallas_call x3 -> x1, Pallas kernels: 171 us -> 153 us  [fused_body(): pl.pallas_call(functools.partial(whole_kernel, size), in_specs=[hbm] * 6...]
where the time goes in v4:
time: 159 us
  Pallas kernels  158 us (99%)
    pallas_call x1, Pallas kernels, fused_body(): pl.pallas_call(functools.partial(whole_kernel, size), in_specs=[hbm] * 6...  153 us
    pallas_call x1, Pallas kernels, fused_body(): pl.pallas_call(functools.partial(unpack_kernel, size.hidden, size.feature...  5.6 us

profile of v4, /device:TPU:1, one launch (start us, length us, event | category | flops | bytes accessed | tf_op | source)
XLA Modules:
  0.0 159.3 jit_solution(5303649639467600711)
XLA Ops:
  0.6 152.9 %shard_map.174 = (f32[8,256,128]{2,1,0:T(8,128)}, f32[10240,128]{1,0:T(8,128)}, bf16[1024,2048]{1,0:T(8,128)(2,1)}, bf16[2048,1024]{1,0:T(8,128)(2,1)}, bf16[102...) custom-call(f32[8,256,128]{2,1,0:T(8,128)} %bitcast.3, f32[8,256,128]{2,1,0:T(8,128)} %bitcast.4, ...), custom_call_target="tpu_custom_call" | custom-call | flops 32212254720 | bytes 33554432 | tf_op jit(solution)/shard_map/pallas_call | solution.py:809
  153.5 5.6 %shard_map.175 = (f32[8,256,128]{2,1,0:T(8,128)}, f32[128,1024]{1,0:T(8,128)}, f32[1024,1024]{1,0:T(8,128)}, f32[1024,128]{1,0:T(8,128)}) custom-call(f32[8,256,128]{2,1,0:T(8,128)} %get-tuple-element.10.f_hbm, f32[10240,128]{1,0:T(8,128)} %get-tuple-element.11.o_hbm), custom_call_target="tpu_custom_call" | custom-call | tf_op jit(solution)/shard_map/pallas_call | solution.py:823

commit v5 on v4

--- a/solution.py
+++ b/solution.py
@@ -165,6 +165,7 @@
 SPAN = CHUNK
 HALF = SPAN // 2
 EARLY = 3
+AHEAD = 2
 LAGS = (0, 1, 3, 5, 7, 9, 11, 13, 14)
 
 
@@ -366,7 +367,7 @@
         self.block = self.pairs * lat_rows
         self.rows = lat_rows * lon
         self.all_pairs = 2 * MW
-        self.degrees = (MW + 1 + 7) // 8 * 8
+        self.degrees = MW
 
 
 class Exchange:
@@ -442,12 +443,18 @@
     mirrored = 2 * first + (lats - 1) - column
     turn = jnp.where(source == jnp.where(north == 1, mirrored, column), 1.0, 0.0).astype(jnp.bfloat16)
     degree = lax.broadcasted_iota(jnp.int32, (size.degrees, width), 0)
+    degree += jnp.where(lax.broadcasted_iota(jnp.int32, (size.degrees, width), 1) >= lats, 1, 0)
     sign = jnp.where(jnp.logical_and(north == 1, lax.rem(degree, 2) == 1), -1.0, 1.0)
-    for i in range(size.couples):
+    for i in range(size.couples + 1):
         table = table_ref[i] * sign
         for value, hi_ref, lo_ref in ((table, plain_hi, plain_lo), (table * quad_ref[...], quad_hi, quad_lo)):
             for part, ref in zip(halves(value), (hi_ref, lo_ref)):
                 ref[i] = plain_dot(part, turn).astype(jnp.bfloat16)
+
+
+def unit(size, table, couple, part):
+    which = size.couples if couple == 0 and part == 1 else couple
+    return table[0][which], table[1][which]
 
 
 def half_sums(size, table, got, swap, couples):
@@ -456,26 +463,26 @@
             jnp.concatenate(
                 [got[pl.ds(4 * i + 2 * w + p, size.half_lats, stride=size.pairs), :] for p in (0, 1)], axis=1)
             for w in (0, 1)], axis=0)
-        coef = split_dot((table[0][i], table[1][i]), value)
         for p in (0, 1):
-            swap.out[pl.ds((2 * i + p) * size.degrees, size.degrees), :] = coef[:, p * LANES:(p + 1) * LANES]
+            swap.out[pl.ds((2 * i + p) * size.degrees, size.degrees), :] = split_dot(
+                unit(size, table, i, p), value[:, p * LANES:(p + 1) * LANES])
         if i < couples:
             swap.start(i)
 
 
-def from_coefs(size, table, swap, exchange):
+def from_coefs(size, table, swap, exchange, begun):
     for i in range(size.couples):
         swap.wait(i)
-        value = jnp.concatenate([
-            swap.out[pl.ds((2 * i + p) * size.degrees, size.degrees), :]
-            + swap.got[pl.ds((2 * i + p) * size.degrees, size.degrees), :] for p in (0, 1)], axis=1)
-        back = split_dot((table[0][i], table[1][i]), value, True)
-        for w in (0, 1):
-            for p in (0, 1):
+        if i + begun < size.couples:
+            swap.start(i + begun)
+        for p in (0, 1):
+            rows = pl.ds((2 * i + p) * size.degrees, size.degrees)
+            back = split_dot(unit(size, table, i, p), swap.out[rows, :] + swap.got[rows, :], True)
+            for w in (0, 1):
                 for d in range(size.team):
                     row = w * size.half_lats + d * size.lat_rows
                     exchange.out[pl.ds(d * size.block + (4 * i + 2 * w + p) * size.lat_rows, size.lat_rows), :] = (
-                        back[row:row + size.lat_rows, p * LANES:(p + 1) * LANES])
+                        back[row:row + size.lat_rows])
         exchange.start(4 * i * size.lat_rows, 4 * size.lat_rows)
 
 
@@ -499,7 +506,7 @@
 def forward_tile(size, row, x, w1, w2, w3, keep):
     h1t, s1_ref, h2t, s2_ref, xt = keep
     rows = x.astype(jnp.bfloat16)
-    span = pl.ds(row, size.lon)
+    span = pl.ds(row, 2 * size.lon)
     if xt is not None:
         xt[:, span] = rows.T
     h1, s1 = silu_pair(jnp.dot(rows, w1[...], preferred_element_type=jnp.float32))
@@ -544,12 +551,15 @@
             put((blocks + 1) * CHUNK + (2 * i + u) * LANES, part[:, u * LANES:(u + 1) * LANES])
 
 
-def weight_gradients(size, h1t, h2t, xt, gt, ga1, ga2, put):
+def weight_gradients(size, h1t, h2t, xt, gt, ga1, ga2, put, between):
+    pieces = size.hidden // LANES // 2
     last_gradient(size, h2t, gt, put)
-
-    @pl.loop(0, size.hidden // LANES // 2)
-    def _(i):
-        middle_gradient(size, h1t, ga2, i, put)
+    for part in range(2):
+        @pl.loop(part * (pieces // 2), (part + 1) * (pieces // 2))
+        def _(i):
+            middle_gradient(size, h1t, ga2, i, put)
+
+        between(part)
 
     first_gradient(size, xt, ga1, put)
 
@@ -608,12 +618,10 @@
     keeps = ((h1t, h1t_hbm, 1), (s1, s1_hbm, 0), (h2t, h2t_hbm, 1), (s2, s2_hbm, 0))
 
     def forward(i, xt, exchange):
-        moved = [
-            forward_tile(size, pl.multiple_of((2 * i + u) * size.lon, size.lon), x[2 * i + u],
-                         w1, w2, w3, (h1t, s1, h2t, s2, xt))
-            for u in (0, 1)
-        ]
-        analyse(size, (ana_hi[...], ana_lo[...]), moved[0], moved[1], 2 * i, exchange.out)
+        moved = forward_tile(size, pl.multiple_of(2 * i * size.lon, 2 * size.lon),
+                             jnp.concatenate([x[2 * i], x[2 * i + 1]], axis=0),
+                             w1, w2, w3, (h1t, s1, h2t, s2, xt))
+        analyse(size, (ana_hi[...], ana_lo[...]), moved[:size.lon], moved[size.lon:], 2 * i, exchange.out)
         start_tile(exchange, i)
 
     @pl.loop(0, tiles)
@@ -629,11 +637,9 @@
             pltpu.make_async_copy(src.at[where], dst.at[where], ksems.at[k]).start()
 
     to_m0.wait()
-    half_sums(size, quads, to_m0.got, swap_m0, size.couples)
-    for i in range(EARLY, size.couples):
-        swap_c.start(i)
-    from_coefs(size, plain, swap_m0, fro_m0)
-    from_coefs(size, quads, swap_c, fro_c)
+    half_sums(size, quads, to_m0.got, swap_m0, AHEAD)
+    from_coefs(size, plain, swap_m0, fro_m0, AHEAD)
+    from_coefs(size, quads, swap_c, fro_c, EARLY)
     for k, (src, dst, _) in enumerate(keeps):
         pltpu.make_async_copy(src, dst, ksems.at[k]).wait()
     fro_m0.wait()
@@ -673,16 +679,16 @@
         g[pl.ds(row, value.shape[0]), :] = value
 
     to_g.wait()
-    half_sums(size, plain, to_g.got, swap_g, size.couples)
-    from_coefs(size, plain, swap_m1, fro_m1)
-    weight_gradients(size, h1t, h2t, xt1, gt, ga1, ga2, keep)
+    half_sums(size, plain, to_g.got, swap_g, AHEAD)
+    from_coefs(size, plain, swap_m1, fro_m1, size.couples)
+    weight_gradients(size, h1t, h2t, xt1, gt, ga1, ga2, keep, lambda i: swap_g.start(AHEAD + i))
     loads[2].start()
     loads[0].start()
     fro_m1.wait()
     synthesise(size, (syn_hi[...], syn_lo[...]), fro_m1.got, store_in(x))
     final_copy = pltpu.make_async_copy(x, final_hbm, fsem)
     final_copy.start()
-    from_coefs(size, quads, swap_g, fro_g)
+    from_coefs(size, quads, swap_g, fro_g, size.couples)
     fro_g.wait()
     synthesise(size, (ant_hi[...], ant_lo[...]), fro_g.got, store_in(c))
 
@@ -706,21 +712,26 @@
             rows = pl.ds(pl.multiple_of((t - LAGS[-1]) * CHUNK, CHUNK), CHUNK)
             pltpu.make_async_copy(red.o.at[rows, :], o_hbm.at[rows, :], osem).start()
 
-        @pl.when(t == 0)
+        @pl.when(t < 2)
         def _():
-            @pl.loop(0, tiles)
+            @pl.loop(t, 1 + t * (blocks // 2 - 1))
             def _(i):
-                span = span_of(i)
-                ga2[span, :] = (mul_t(gt[span, :], w3[...]) * s2[span, :].astype(jnp.float32)).astype(jnp.bfloat16)
+                columns = pl.ds(pl.multiple_of(i * 2 * LANES, 2 * LANES), 2 * LANES)
+                ga2[:, columns] = (mul_t(gt[...], w3[columns, :]) * s2[:, columns].astype(jnp.float32)
+                                   ).astype(jnp.bfloat16)
 
         @pl.when(jnp.logical_and(lax.rem(t, 2) == 0, t < blocks))
         def _():
             middle_gradient(size, h1t, ga2, t // 2, put)
 
-        @pl.when(jnp.logical_and(lax.rem(t, 2) == 1, t < 2 * tiles))
+        @pl.when(jnp.logical_and(lax.rem(t, 2) == 1, jnp.logical_and(t > 1, t < blocks)))
         def _():
-            span = span_of(t // 2)
-            ga1[span, :] = (mul_t(ga2[span, :], w2[...]) * s1[span, :].astype(jnp.float32)).astype(jnp.bfloat16)
+            first = t // 2 - 1
+
+            @pl.loop(first, jnp.where(t == blocks - 1, tiles, first + 1))
+            def _(i):
+                span = span_of(i)
+                ga1[span, :] = (mul_t(ga2[span, :], w2[...]) * s1[span, :].astype(jnp.float32)).astype(jnp.bfloat16)
 
         @pl.when(t == blocks)
         def _():
@@ -770,15 +781,27 @@
 def packed_tables(size):
     table, quad = legendre_tables(size.lats, MW)
     lats = size.half_lats
-    packed = np.zeros((size.team, size.couples, size.degrees, 2 * lats), np.float32)
+    packed = np.zeros((size.team, size.couples + 1, size.degrees, 2 * lats), np.float32)
     order = []
+
+    def fill(out, wave, other, rows):
+        out[:rows, :lats] = table[wave, :rows, :lats]
+        if rows < MW:
+            out[rows:, lats:] = table[other, MW - 1 - rows::-1, :lats]
+
     for d in range(size.team):
         for i in range(size.couples):
             m = d + size.team * i
-            other = MW - 1 - m
-            packed[d, i, :MW - m, :lats] = table[m, :MW - m, :lats]
-            packed[d, i, MW - m:MW + 1, lats:] = table[other, m::-1, :lats]
-            order += [2 * m, 2 * m + 1, 2 * other, 2 * other + 1]
+            if m == 0:
+                middle = MW // 2
+                fill(packed[d, i], 0, 0, MW)
+                fill(packed[d, size.couples], middle, middle, middle)
+                order += [0, 2 * middle, 1, 2 * middle + 1]
+                continue
+            fill(packed[d, i], m, MW - m, MW - m)
+            if i == 0:
+                packed[d, size.couples] = packed[d, 0]
+            order += [2 * m, 2 * m + 1, 2 * (MW - m), 2 * (MW - m) + 1]
     return packed, np.concatenate([quad[:lats]] * 2)[None, :], np.asarray(order)
 
 
@@ -801,7 +824,7 @@
     grads = jax.ShapeDtypeStruct(((size.hidden // LANES + 2) * CHUNK, LANES), f32)
     buf = lambda shape: pltpu.VMEM(shape.shape, shape.dtype)
     dma = pltpu.SemaphoreType.DMA
-    packed = (size.couples, size.degrees, 2 * size.half_lats)
+    packed = (size.couples + 1, size.degrees, 2 * size.half_lats)
     tables = [pltpu.VMEM(packed, f32)] + [pltpu.VMEM(packed, bf16)] * 4
     narrow = pltpu.VMEM((size.rows, LANES), bf16)
     x_t = pltpu.VMEM((LANES, size.rows), bf16)

time: 159 us -> 154 us (0.969)
  Pallas kernels: 158 us -> 153 us
    pallas_call x1, Pallas kernels: 153 us -> 147 us  [fused_body(): pl.pallas_call(functools.partial(whole_kernel, size), in_specs=[hbm] * 6...]
where the time goes in v5:
time: 154 us; the launch traced here: 153 us
  Pallas kernels  153 us (99%)
    pallas_call x1, Pallas kernels, fused_body(): pl.pallas_call(functools.partial(whole_kernel, size), in_specs=[hbm] * 6...  147 us
    pallas_call x1, Pallas kernels, fused_body(): pl.pallas_call(functools.partial(unpack_kernel, size.hidden, size.feature...  5.6 us

profile of v5, /device:TPU:1, one launch (start us, length us, event | category | flops | bytes accessed | tf_op | source)
XLA Modules:
  0.0 153.4 jit_solution(15421578824996076059)
XLA Ops:
  0.6 147.0 %shard_map.174 = (f32[8,256,128]{2,1,0:T(8,128)}, f32[10240,128]{1,0:T(8,128)}, bf16[1024,2048]{1,0:T(8,128)(2,1)}, bf16[2048,1024]{1,0:T(8,128)(2,1)}, bf16[102...) custom-call(f32[8,256,128]{2,1,0:T(8,128)} %bitcast.3, f32[8,256,128]{2,1,0:T(8,128)} %bitcast.4, ...), custom_call_target="tpu_custom_call" | custom-call | flops 32212254720 | bytes 33554432 | tf_op jit(solution)/shard_map/pallas_call | solution.py:832
  147.7 5.6 %shard_map.175 = (f32[8,256,128]{2,1,0:T(8,128)}, f32[128,1024]{1,0:T(8,128)}, f32[1024,1024]{1,0:T(8,128)}, f32[1024,128]{1,0:T(8,128)}) custom-call(f32[8,256,128]{2,1,0:T(8,128)} %get-tuple-element.10.f_hbm, f32[10240,128]{1,0:T(8,128)} %get-tuple-element.11.o_hbm), custom_call_target="tpu_custom_call" | custom-call | tf_op jit(solution)/shard_map/pallas_call | solution.py:846
